TPU v7x, 128 devices: a whole 4x4x4 slice. The times are simulated.
128 devices in a mesh: gx: 8 (over z, core), gy: 16 (over x, y).
Axes of the slice: x: 4, y: 4, z: 4, core: 2. Of those that a mesh axis runs over, the one named last changes fastest.
Arguments:
- policy_logp: float32 [16, 2048, 4096], P('gy', 'gx'), may hold values from -2 to 0
- anchor_logp: float32 [16, 2048, 4096], P('gy', 'gx'), may hold values from -2 to 0
- lengths: int32 [16, 2048], P('gy', 'gx'), may hold values from 512 to 4096
- rewards: int32 [16, 2048], P('gy', 'gx'), may hold values from 0 to 8
- slot_prompt: int32 [16, 2048], P('gy', 'gx'), may hold values from 0 to 2047, as said below
Outputs:
- token_grad: float32 [16, 2048, 4096], P(None, ('gx', 'gy'))
- sample_loss: float32 [16, 2048], P(None, ('gx', 'gy'))
- advantage: float32 [16, 2048], P(None, ('gx', 'gy'))
Inputs may be any that keep to these rules, and one draw needn't show every extreme that they name: `slot_prompt`: for every member k and every aligned block of 256 slots, the slots of the block hold each prompt of the same block exactly once.
All inputs are finite; a program needn't handle non-finite values.
Results may differ from a plain program's by a relative error of at most 0.00002.
Values sent between devices are 32-bit elements; how exact they have to be, the bound alone decides.
No kernel may reach another device: no remote copies, remote signals or barrier semaphores. Data moves between devices by JAX's collectives and lax.ppermute only.
A program may use at most 64 MiB of HBM per device.

v0:
```python
import jax
import jax.numpy as jnp
from jax import lax
from jax.sharding import Mesh
from jax.sharding import PartitionSpec as P

GX_GY = ("gx_0", "gx_1", "gy_0", "gy_1")
GY = ("gy_0", "gy_1")
GX = ("gx_0", "gx_1")


kl_weight = 0.1


def by_axis(x, axes):
    for axis in axes:
        x = lax.psum(x, axis)
    return x


def sent_together(arrays, axis, split_dim, concat_dim, along):
    columns = [a.reshape(*a.shape[:along], -1) for a in arrays]
    both = jnp.concatenate(columns, axis=along)
    out, at, gathered = (
        lax.all_to_all(both, axis, split_axis=split_dim, concat_axis=concat_dim, tiled=True),
        0,
        [],
    )
    for a, column in zip(arrays, columns):
        piece = out[..., at : at + column.shape[along]]
        gathered.append(piece.reshape(*piece.shape[:along], *a.shape[along:]))
        at += column.shape[along]
    return tuple(gathered)


def score_tokens(policy, anchor, seq_len, reward, total, members, grad_scale, loss_scale):
    advantage = (members * reward - total[None, :]) / (members - 1)
    positions = lax.broadcasted_iota(jnp.float32, policy.shape, 2)
    valid = positions < seq_len[:, :, None]
    log_ratio = anchor - policy
    ratio = jnp.exp(log_ratio)
    token_term = -advantage[:, :, None] * policy + kl_weight * (ratio - log_ratio - 1.0)
    token_grad = (
        jnp.where(valid, -advantage[:, :, None] + kl_weight * (1.0 - ratio), 0.0) * grad_scale
    )
    sample_loss = jnp.sum(jnp.where(valid, token_term, 0.0), axis=2) * loss_scale
    return (token_grad, sample_loss, advantage)


def body(policy_logp, anchor_logp, lengths, rewards, slot_prompt):
    members_dev, slots, seq_slots = policy_logp.shape
    local_prompt = slot_prompt % slots
    member_rows = lax.broadcasted_iota(jnp.int32, (members_dev, slots), 0)
    slot_ids = lax.broadcasted_iota(jnp.int32, (members_dev, slots), 1)
    inverse = jnp.zeros((members_dev, slots), jnp.int32).at[member_rows, local_prompt].set(slot_ids)
    sorted_policy = jnp.take_along_axis(policy_logp, inverse[:, :, None], axis=1)
    sorted_anchor = jnp.take_along_axis(anchor_logp, inverse[:, :, None], axis=1)
    sorted_len = jnp.take_along_axis(lengths, inverse, axis=1).astype(jnp.float32)
    sorted_reward = jnp.take_along_axis(rewards, inverse, axis=1).astype(jnp.float32) * 0.25
    count_local = jnp.sum(lengths.astype(jnp.float32))
    token_total = by_axis(count_local, GX_GY)
    members = members_dev * lax.axis_size(GY)
    samples = members * slots * lax.axis_size(GX)
    grad_scale = samples * seq_slots / token_total
    loss_scale = samples / token_total
    member_sums = jnp.sum(sorted_reward, axis=0)
    total = by_axis(member_sums, GY)
    token_grad, sample_loss, advantage = score_tokens(
        sorted_policy,
        sorted_anchor,
        sorted_len,
        sorted_reward,
        total,
        members,
        grad_scale,
        loss_scale,
    )
    return sent_together((token_grad, sample_loss, advantage), GY, 1, 0, 2)


def solution(mesh):
    torus = Mesh(mesh.devices.reshape(4, 2, 4, 4), ("gx_0", "gx_1", "gy_0", "gy_1"))
    return jax.shard_map(
        body,
        mesh=torus,
        in_specs=(P(GY, GX, None), P(GY, GX, None), P(GY, GX), P(GY, GX), P(GY, GX)),
        out_specs=(P(None, GX_GY, None), P(None, GX_GY), P(None, GX_GY)),
        check_vma=False,
    )
```

profile of v0, /device:TPU:0, one launch (start us, length us, event | category | flops | bytes accessed | tf_op | source)
XLA Modules:
  0.0 137.0 jit_solution(9556072892073195460)
XLA Ops:
  0.6 0.0 copy-start
  0.6 1.3 convert_reduce_fusion
  1.9 12.5 %psum.44 = f32[]{:T(128)} all-reduce(f32[]{:T(128)} %convert_reduce_fusion), channel_id=1, replica_groups=mesh['gx_0'=4,'gx_1'=2,'gy_0'=4,'gy_1'=4] {'gx_0'}, use_global_device_ids=true, to_apply=%region_4.7 | all-reduce | flops 1 | bytes 8 | tf_op jit(solution)/shard_map/psum | solution.py:17
  14.4 3.1 %psum.45 = f32[]{:T(128)} all-reduce(f32[]{:T(128)} %psum.44), channel_id=1, replica_groups=mesh['gx_0'=4,'gx_1'=2,'gy_0'=4,'gy_1'=4] {'gx_1'}, use_global_device_ids=true, to_apply=%region_5.8 | all-reduce | flops 1 | bytes 8 | tf_op jit(solution)/shard_map/psum | solution.py:17
  17.5 0.7 fusion.11
  18.2 1.4 %scatter_custom_fusion = s32[256]{0:T(256)S(1)} fusion(s32[256]{0:T(256)S(1)} %bitcast.61, s32[256]{0:T(256)S(1)} %iota.12, s32[]{:T(128)} %constant.18.clone.1), kind=kCustom, calls=%fused_computation.40 | custom fusion | bytes 1028 | tf_op jit(solution)/shard_map/scatter | solution.py:55
  19.7 0.0 copy-done
  19.7 1.9 %gather_fusion.1 = s32[256]{0:T(256)S(1)} fusion(s32[256]{0:T(256)S(1)} %bitcast.41, s32[1024]{0:T(1024)S(1)} %pad_clamp_fusion.1), kind=kCustom, calls=%fused_computation.2.clone | custom fusion | bytes 3072 | tf_op jit(solution)/shard_map/jit(take_along_axis)/gather | solution.py:59
  21.7 2.0 %gather_fusion = s32[256]{0:T(256)S(1)} fusion(s32[256]{0:T(256)} %bitcast.42, s32[1024]{0:T(1024)S(1)} %pad_clamp_fusion.1), kind=kCustom, calls=%fused_computation.clone | custom fusion | bytes 3072 | tf_op jit(solution)/shard_map/jit(take_along_axis)/gather | solution.py:58
  23.7 11.1 %all-reduce.2 = (f32[]{:T(128)}, f32[256]{0:T(256)S(1)}) all-reduce(f32[]{:T(128)} %psum.45, f32[256]{0:T(256)S(1)} %bitcast.62), channel_id=1, replica_groups=mesh['gx_0'=4,'gx_1'=2,'gy_0'=4,'gy_1'=4] {'gy_0'}, use_global_device_ids=true, to_apply=%region_6.9 | all-reduce | flops 257 | bytes 2056 | tf_op jit(solution)/shard_map/psum | solution.py:17
  34.8 11.3 %all-reduce.1 = (f32[]{:T(128)}, f32[1,256]{1,0:T(1,128)S(1)}) all-reduce(f32[]{:T(128)} %get-tuple-element.9, f32[1,256]{1,0:T(1,128)S(1)} %bitcast.63), channel_id=1, replica_groups=mesh['gx_0'=4,'gx_1'=2,'gy_0'=4,'gy_1'=4] {'gy_1'}, use_global_device_ids=true, to_apply=%region_7.10 | all-reduce | flops 257 | bytes 2056 | tf_op jit(solution)/shard_map/psum | solution.py:17
  47.5 0.1 copy.23
  47.7 7.9 %gather_fusion.3 = f32[256,4096]{1,0:T(8,128)} fusion(f32[256,4096]{1,0:T(8,128)} %bitcast.43, s32[1024]{0:T(1024)S(1)} %pad_clamp_fusion), kind=kCustom, calls=%fused_computation.3.clone | custom fusion | bytes 8389632 | tf_op jit(solution)/shard_map/jit(take_along_axis)/gather | solution.py:56
  55.6 7.8 %gather_fusion.2 = f32[256,4096]{1,0:T(8,128)} fusion(f32[256,4096]{1,0:T(8,128)} %bitcast.44, s32[1024]{0:T(1024)S(1)} %pad_clamp_fusion), kind=kCustom, calls=%fused_computation.1.clone | custom fusion | bytes 8389632 | tf_op jit(solution)/shard_map/jit(take_along_axis)/gather | solution.py:57
  63.4 6.4 %fusion.8 = (f32[256]{0:T(256)S(1)}, f32[1,256,4096]{2,1,0:T(8,128)}) fusion(f32[256,4096]{1,0:T(8,128)} %gather_fusion.3, f32[256,4096]{1,0:T(8,128)} %gather_fusion.2, f32[256]{0:T(256)S(1)} %bitcast.55, f32[256]{0:T(256)S(1)} %bitcast.54, pred[256]{0:T(512)(128)(4,1)S(1)} %get-tuple-element.11, f32[]{:T(128)S(6)} %div.14), kind=kLoop, calls=%fused_computation.15 | loop fusion | flops 16776960 | bytes 12586244 | tf_op jit(solution)/shard_map/reduce_sum | solution.py:46
  69.7 0.1 copy.22
  69.9 5.6 %concatenate.7 = f32[1,256,4098]{2,1,0:T(8,128)} concatenate(f32[1,256,4096]{2,1,0:T(8,128)} %get-tuple-element.16, f32[1,256,1]{2,1,0:T(8,128)S(1)} %copy.22, f32[1,256,1]{2,1,0:T(8,128)S(1)} %copy.23), dimensions={2} | concatenate | bytes 8392704 | tf_op jit(solution)/shard_map/concatenate | solution.py:23
  75.5 6.7 %copy.24 = f32[1,256,4098]{2,0,1:T(1,128)S(1)} copy(f32[1,256,4098]{2,1,0:T(8,128)} %concatenate.7) | data formatting | bytes 8392704 | tf_op jit(solution)/shard_map/concatenate | solution.py:23
  82.1 51.2 %all_to_all.12 = f32[1,256,4098]{2,0,1:T(1,128)S(1)} all-to-all(f32[1,256,4098]{2,0,1:T(1,128)S(1)} %copy.24), channel_id=1, replica_groups=mesh['gx_0'=4,'gx_1'=2,'gy_0'=4,'gy_1'=4] {'gy_0','gy_1'}, dimensions={1} | all-to-all | bytes 8392704 | tf_op jit(solution)/shard_map/all_to_all | solution.py:25
  133.4 0.3 copy.25
  133.7 0.8 slice_reduce_fusion
  134.5 2.5 %slice.24 = f32[16,16,4096]{2,1,0:T(8,128)} slice(f32[16,16,4098]{2,1,0:T(8,128)S(1)} %bitcast.46), slice={[0:16], [0:16], [0:4096]} | slice | bytes 8388608 | tf_op jit(solution)/shard_map/slice | solution.py:30
  (11 shorter events, 0.1 us)
Async XLA Ops:
  0.6 19.1 %copy-start = (s32[1,256]{1,0:T(1,128)S(1)}, s32[1,256]{1,0:T(1,128)}, u32[]{:S(2)}) copy-start(s32[1,256]{1,0:T(1,128)} %param.12) | copy-start | bytes 3076
where the time goes:
time: 138 us; the launch traced here: 137 us
  blocking collectives  89.3 us (65%)
  local copies, waits for them, and re-layouts  37.2 us (27%)
  other arithmetic  8.42 us (6%)
  between operations  2.11 us (2%)
    all_to_all x1, blocking collectives, sent_together(): lax.all_to_all(both, axis, split_axis=split_dim, concat_axis=concat_dim,...  51.2 us
    psum x4, blocking collectives, by_axis(): x = lax.psum(x, axis)  38 us
    concatenate x2, local copies, waits for them, and re-layouts, sent_together(): both = jnp.concatenate(columns, axis=along)  12.2 us
    gather x1, local copies, waits for them, and re-layouts, body(): jnp.take_along_axis(policy_logp, inverse[:, :, None], axis=1)  7.89 us
    gather x1, local copies, waits for them, and re-layouts, body(): jnp.take_along_axis(anchor_logp, inverse[:, :, None], axis=1)  7.8 us
    reduce_sum x1, other arithmetic, score_tokens(): jnp.sum(jnp.where(valid, token_term, 0.0), axis=2) * loss_scale  6.36 us
    slice x2, local copies, waits for them, and re-layouts, sent_together(): piece = out[..., at:at + column.shape[along]]  3.33 us

commit v1 on v0

v1 whole, which is shorter than its diff:
```python
import jax
import jax.numpy as jnp
from jax import lax
from jax.experimental import pallas as pl
from jax.experimental.pallas import tpu as pltpu
from jax.sharding import Mesh
from jax.sharding import PartitionSpec as P

GX_GY = ("gx_0", "gx_1", "gy_0", "gy_1")
GY = ("gy_0", "gy_1")
GX = ("gx_0", "gx_1")

KL = 0.1
LANES = 128
META = 8
FAST = 432


def lane_rows(x, rows, width):
    return (
        x.reshape(rows // 8, 8, width // LANES, LANES)
        .transpose(0, 2, 1, 3)
        .reshape(rows * width // LANES, LANES)
    )


def pack_kernel(
    dests,
    per_dest,
    cols,
    len_ref,
    prompt_ref,
    vec_ref,
    tok_ref,
    policy_hbm,
    anchor_hbm,
    main_hbm,
    rest_hbm,
    policy,
    anchor,
    stage,
    part_p,
    part_q,
    meta,
    len_of,
    slot_of,
    in_sem,
    out_sem,
):
    slots = dests * per_dest
    full = META + per_dest * cols
    head = META + FAST
    loads = [
        pltpu.make_async_copy(policy_hbm, policy, in_sem.at[0]),
        pltpu.make_async_copy(anchor_hbm, anchor, in_sem.at[1]),
    ]
    for load in loads:
        load.start()

    @pl.loop(0, slots)
    def _(s):
        p = lax.rem(prompt_ref[0, s], slots)
        len_of[p] = len_ref[0, s]
        slot_of[p] = s

    ids = lax.broadcasted_iota(jnp.int32, (slots, slots), 0)
    pick = jnp.where(lax.rem(vec_ref[2:3, :], slots) == ids, 1.0, 0.0)
    values = vec_ref[0:8, :].astype(jnp.float32)
    ordered = lax.dot_general(
        values,
        pick,
        (((1,), (1,)), ((), ())),
        precision=lax.Precision.HIGHEST,
        preferred_element_type=jnp.float32,
    )
    position = lax.broadcasted_iota(jnp.int32, (cols, LANES), 0) * LANES + lax.broadcasted_iota(
        jnp.int32, (cols, LANES), 1
    )
    for load in loads:
        load.wait()

    def out_copies(dest, slot):
        return (
            pltpu.make_async_copy(
                stage.at[slot, pl.ds(0, head)], main_hbm.at[dest], out_sem.at[0, slot]
            ),
            pltpu.make_async_copy(
                stage.at[slot, pl.ds(head, full - head)], rest_hbm.at[dest], out_sem.at[1, slot]
            ),
        )

    for dest in range(dests):

        def row(r, carry):
            at, dest = carry
            p = dest * per_dest + r
            s = slot_of[p]
            length = len_of[p]
            first = lax.div(s, 8) * (8 * cols) + lax.rem(s, 8)
            a = policy[pl.ds(first, cols, stride=8), :]
            d = anchor[pl.ds(first, cols, stride=8), :] - a
            e = jnp.exp(d)
            valid = position < length
            stage[dest, pl.ds(at, cols), :] = jnp.where(valid, KL * (1.0 - e), 0.0)
            term_p = jnp.where(valid, a, 0.0)
            term_q = jnp.where(valid, KL * (e - d - 1.0), 0.0)
            part_p[p, :, :] = jnp.sum(term_p.reshape(cols // 8, 8, LANES), axis=0)
            part_q[p, :, :] = jnp.sum(term_q.reshape(cols // 8, 8, LANES), axis=0)
            return at + lax.div(length + (LANES - 1), LANES), dest

        lax.fori_loop(0, per_dest, row, (META, dest), unroll=4)

    ones = jnp.full((8, LANES), 1.0, jnp.float32)

    def lanes(part):
        return lax.dot_general(
            ones,
            jnp.sum(part[...], axis=1),
            (((1,), (1,)), ((), ())),
            precision=lax.Precision.HIGHEST,
            preferred_element_type=jnp.float32,
        )[0:1]

    rows_of = jnp.floor((ordered[0:1] + (LANES - 1.0)) * (1.0 / LANES))
    sums_p, sums_q = lanes(part_p), lanes(part_q)
    tokens = jnp.full((1, LANES), 1.0, jnp.float32) * tok_ref[0, 0]
    meta[4:5, :] = tokens
    group = lax.broadcasted_iota(jnp.int32, (1, slots), 1)
    most = jnp.zeros((1, 1), jnp.float32)
    for dest in range(dests):
        inside = (group >= dest * per_dest) & (group < (dest + 1) * per_dest)
        most = jnp.maximum(most, jnp.sum(jnp.where(inside, rows_of, 0.0), axis=1, keepdims=True))
    for dest in range(dests):
        half = dest * per_dest // LANES * LANES
        stage[dest, 0:1, :] = ordered[0:1, half : half + LANES]
        stage[dest, 1:2, :] = ordered[1:2, half : half + LANES]
        stage[dest, 2:3, :] = sums_p[:, half : half + LANES]
        stage[dest, 3:4, :] = sums_q[:, half : half + LANES]
        stage[dest, 4:5, :] = tokens
        stage[dest, 5:8, :] = jnp.broadcast_to(most, (3, LANES))
        for copy in out_copies(dest, dest):
            copy.start()
    for dest in range(dests):
        for copy in out_copies(dest, dest):
            copy.wait()


def pack(lengths, prompts, vec, tokens, policy, anchor, dests):
    slots = lengths.shape[1]
    per_dest = slots // dests
    cols = policy.shape[0] // slots
    full = META + per_dest * cols
    head = META + FAST
    smem = pl.BlockSpec(memory_space=pltpu.SMEM)
    hbm = pl.BlockSpec(memory_space=pl.ANY)

    def body(*refs):
        pack_kernel(dests, per_dest, cols, *refs)

    return pl.pallas_call(
        body,
        out_shape=(
            jax.ShapeDtypeStruct((dests, head, LANES), jnp.float32),
            jax.ShapeDtypeStruct((dests, full - head, LANES), jnp.float32),
        ),
        in_specs=[smem, smem, pl.BlockSpec(memory_space=pltpu.VMEM), smem, hbm, hbm],
        out_specs=(hbm, hbm),
        scratch_shapes=[
            pltpu.VMEM((slots * cols, LANES), jnp.float32),
            pltpu.VMEM((slots * cols, LANES), jnp.float32),
            pltpu.VMEM((dests, full + cols, LANES), jnp.float32),
            pltpu.VMEM((slots, 8, LANES), jnp.float32),
            pltpu.VMEM((slots, 8, LANES), jnp.float32),
            pltpu.VMEM((8, LANES), jnp.float32),
            pltpu.SMEM((slots,), jnp.int32),
            pltpu.SMEM((slots,), jnp.int32),
            pltpu.SemaphoreType.DMA((2,)),
            pltpu.SemaphoreType.DMA((2, dests)),
        ],
        name="pack",
    )(lengths, prompts, vec, tokens, policy, anchor)


def score_kernel(
    members,
    per_dest,
    cols,
    scales,
    parts,
    refs,
):
    (
        *got_hbm,
        grad_hbm,
        loss_ref,
        adv_ref,
        got,
        grad,
        meta,
        numbers,
        rows_at,
        got_sem,
        num_sem,
        out_sem,
    ) = refs
    grad_scale, loss_scale = scales
    width = per_dest * cols

    def in_copies(k):
        at, copies = 0, []
        for i, (part, size) in enumerate(zip(got_hbm, parts)):
            copies.append(
                pltpu.make_async_copy(part.at[k], got.at[k, pl.ds(at, size)], got_sem.at[i, k])
            )
            at += size
        return copies

    heads = [
        pltpu.make_async_copy(got_hbm[0].at[k, pl.ds(0, META)], meta.at[k], num_sem.at[k])
        for k in range(members)
    ]
    for copy in heads:
        copy.start()
    for k in range(members):
        for copy in in_copies(k):
            copy.start()
    for copy in heads:
        copy.wait()

    def field(i):
        return jnp.concatenate([meta[k, i : i + 1, :] for k in range(members)], axis=0)

    reward = field(1) * 0.25
    total = jnp.sum(reward, axis=0, keepdims=True)
    advantage = (members * reward - total) / (members - 1)
    tokens = jnp.sum(field(4), axis=0, keepdims=True)
    loss = (field(3) - advantage * field(2)) * (loss_scale / tokens)
    mine = lax.axis_index(GY)
    start = lax.rem(mine * per_dest, LANES)
    shift = lax.rem(LANES - start, LANES)
    loss_ref[...] = pltpu.roll(loss, shift, 1)[:, 0:per_dest]
    adv_ref[...] = pltpu.roll(advantage, shift, 1)[:, 0:per_dest]
    rows_at[0] = pltpu.roll(field(0), shift, 1)
    rows_at[1] = pltpu.roll(advantage, shift, 1)
    rows_at[2] = jnp.broadcast_to(grad_scale / tokens, (members, LANES))
    to_scalars = pltpu.make_async_copy(rows_at, numbers, num_sem.at[members])
    to_scalars.start()
    to_scalars.wait()
    scale = numbers[2, 0, 0]
    position = lax.broadcasted_iota(jnp.int32, (cols, LANES), 0) * LANES + lax.broadcasted_iota(
        jnp.int32, (cols, LANES), 1
    )

    def out_copy(k):
        return pltpu.make_async_copy(
            grad.at[pl.ds(k * width, width)], grad_hbm.at[pl.ds(k * width, width)], out_sem.at[k]
        )

    @pl.loop(0, members)
    def _(k):
        for copy in in_copies(k):
            copy.wait()

        def row(r, at):
            length = numbers[0, k, r].astype(jnp.int32)
            x = got[k, pl.ds(at, cols), :]
            y = jnp.where(position < length, x - numbers[1, k, r], 0.0) * scale
            first = k * width + lax.div(r, 8) * (8 * cols) + lax.rem(r, 8)
            grad[pl.ds(first, cols, stride=8), :] = y
            return at + lax.div(length + (LANES - 1), LANES)

        lax.fori_loop(0, per_dest, row, META, unroll=4)
        out_copy(k).start()

    @pl.loop(0, members)
    def _(k):
        out_copy(k).wait()


def score(got, scales, per_dest, cols):
    members = got[0].shape[0]
    parts = [g.shape[1] for g in got]
    full = META + per_dest * cols
    hbm = pl.BlockSpec(memory_space=pl.ANY)
    vmem = pl.BlockSpec(memory_space=pltpu.VMEM)

    def body(*refs):
        score_kernel(members, per_dest, cols, scales, parts, refs)

    small = jax.ShapeDtypeStruct((members, per_dest), jnp.float32)
    return pl.pallas_call(
        body,
        out_shape=(
            jax.ShapeDtypeStruct((members * per_dest * cols, LANES), jnp.float32),
            small,
            small,
        ),
        in_specs=[hbm] * len(got),
        out_specs=(hbm, vmem, vmem),
        scratch_shapes=[
            pltpu.VMEM((members, full + cols, LANES), jnp.float32),
            pltpu.VMEM((members * per_dest * cols, LANES), jnp.float32),
            pltpu.VMEM((members, META, LANES), jnp.float32),
            pltpu.SMEM((3, members, LANES), jnp.float32),
            pltpu.VMEM((3, members, LANES), jnp.float32),
            pltpu.SemaphoreType.DMA((len(got), members)),
            pltpu.SemaphoreType.DMA((members + 1,)),
            pltpu.SemaphoreType.DMA((members,)),
        ],
        name="score",
    )(*got)


def over_gx(x):
    for axis, size in (("gx_0", lax.axis_size("gx_0")), ("gx_1", lax.axis_size("gx_1"))):
        step = 1
        while step < size:
            x = x + lax.ppermute(x, axis, [(i, i ^ step) for i in range(size)])
            step *= 2
    return x


def body(policy_logp, anchor_logp, lengths, rewards, slot_prompt):
    members_dev, slots, seq_slots = policy_logp.shape
    dests = lax.axis_size(GY)
    per_dest = slots // dests
    cols = seq_slots // LANES
    members = members_dev * dests
    samples = members * slots * lax.axis_size(GX)
    scales = (float(samples * seq_slots), float(samples))
    tokens = over_gx(jnp.sum(lengths.astype(jnp.float32)).reshape(1, 1))
    vec = jnp.concatenate([lengths, rewards, slot_prompt] + [slot_prompt] * 5, axis=0)
    main, rest = pack(
        lengths,
        slot_prompt,
        vec,
        tokens,
        lane_rows(policy_logp, slots, seq_slots),
        lane_rows(anchor_logp, slots, seq_slots),
        dests,
    )
    main = lax.all_to_all(main, GY, 0, 0, tiled=True)
    most = jnp.max(main[:, 5, 0])

    def all_there(main, rest):
        return score((main,), scales, per_dest, cols)

    def more_to_come(main, rest):
        rest = lax.all_to_all(rest, GY, 0, 0, tiled=True)
        return score((main, rest), scales, per_dest, cols)

    grad, loss, advantage = lax.cond(most <= FAST, all_there, more_to_come, main, rest)
    grad = (
        grad.reshape(members, per_dest // 8, cols, 8, LANES)
        .transpose(0, 1, 3, 2, 4)
        .reshape(members, per_dest, seq_slots)
    )
    return grad, loss, advantage


def solution(mesh):
    torus = Mesh(mesh.devices.reshape(4, 2, 4, 4), ("gx_0", "gx_1", "gy_0", "gy_1"))
    return jax.shard_map(
        body,
        mesh=torus,
        in_specs=(P(GY, GX, None), P(GY, GX, None), P(GY, GX), P(GY, GX), P(GY, GX)),
        out_specs=(P(None, GX_GY, None), P(None, GX_GY), P(None, GX_GY)),
        check_vma=False,
    )
```

time: 138 us -> 89 us (0.64)
  blocking collectives: 89.3 us -> 51.9 us
  local copies, waits for them, and re-layouts: 37.2 us -> 3.28 us
  Pallas kernels: 0 us -> 18.8 us
  starting transfers between devices: 0 us -> 8.29 us
  other arithmetic: 8.42 us -> 1.9 us
  between operations: 2.11 us -> 3.85 us
    psum x4 -> x0, blocking collectives: 38 us -> none  [by_axis(): x = lax.psum(x, axis)]
    gather x4 -> x0, local copies, waits for them, and re-layouts: 19.6 us -> none  [the longest x1 7.89 us: body(): jnp.take_along_axis(policy_logp, inverse[:, :, None], axis=1)]
    pallas_call x0 -> x2, Pallas kernels: none -> 18.8 us  [the longest x1 11 us: pack(): pl.pallas_call(body, out_shape=(jax.ShapeDtypeStruct((dests, head, LANES)...]
    concatenate x3 -> x1, local copies, waits for them, and re-layouts: 12.2 us -> 1.51 us  [body(): jnp.concatenate([lengths, rewards, slot_prompt] + [slot_prompt] * 5, axis=0)]
    ppermute x0 -> x3, starting transfers between devices: none -> 8.29 us  [over_gx(): x = x + lax.ppermute(x, axis, [(i, i ^ step) for i in range(size)])]
    reduce_sum x2 -> x1, other arithmetic: 7.65 us -> 1.29 us  [body(): tokens = over_gx(jnp.sum(lengths.astype(jnp.float32)).reshape(1, 1))]
    slice x2 -> x0, local copies, waits for them, and re-layouts: 3.33 us -> none  [sent_together(): piece = out[..., at:at + column.shape[along]]]
    unnamed x3 -> x2, local copies, waits for them, and re-layouts: 0.29 us -> 1.76 us
  transfers between devices with their start and end apart: 0 -> 3, of which waited for: 0 -> 3; matrix products, arithmetic and copies ran while one was open for 0% -> 2% of each run, Pallas kernels for 0% -> 0%
where the time goes in v1:
time: 89 us; the launch traced here: 88.7 us
  blocking collectives  51.9 us (58%)
  Pallas kernels  18.8 us (21%)
  starting transfers between devices  8.29 us (9%)
  between operations  3.85 us (4%)
  local copies, waits for them, and re-layouts  3.28 us (4%)
  other arithmetic  1.9 us (2%)
    all_to_all x1, blocking collectives, body(): main = lax.all_to_all(main, GY, 0, 0, tiled=True)  51.9 us
    pallas_call x1, Pallas kernels, pack(): pl.pallas_call(body, out_shape=(jax.ShapeDtypeStruct((dests, head, LANES)...  11 us
    ppermute x3, starting transfers between devices, over_gx(): x = x + lax.ppermute(x, axis, [(i, i ^ step) for i in range(size)])  8.29 us
    pallas_call x1, Pallas kernels, score(): pl.pallas_call(body, out_shape=(jax.ShapeDtypeStruct((members * per_dest...  7.84 us
  transfers between devices with their start and end apart: 3, of which 3 were waited for; matrix products, arithmetic and copies ran while one was open for 2% of the time, Pallas kernels for 0%

profile of v1, /device:TPU:0, one launch (start us, length us, event | category | flops | bytes accessed | tf_op | source)
XLA Modules:
  0.0 88.7 jit_solution(3014834412754353379)
XLA Ops:
  0.6 1.3 %convert_reduce_fusion = f32[]{:T(128)} fusion(s32[1,256]{1,0:T(1,128)} %refs_0_.2), kind=kLoop, calls=%fused_computation.1 | loop fusion | flops 511 | bytes 1028 | tf_op jit(solution)/shard_map/reduce_sum | solution.py:331
  1.9 2.0 %collective-permute-start = (f32[1,1]{1,0:T(1,128)}, f32[1,1]{1,0:T(1,128)}, u32[]{:S(2)}, u32[]{:S(2)}) collective-permute-start(f32[1,1]{1,0:T(1,128)} %bitcast), channel_id=1, source_target_pairs={{0,32},{32,0},{64,96},{96,64},{1,33},{33,1},{65,97},{97,65},{2,34}... | collective-permute-start | bytes 20 | tf_op jit(solution)/shard_map/ppermute | solution.py:318
  3.9 1.5 %concatenate.3.refs_2_ = s32[8,256]{1,0:T(8,128)} concatenate(s32[1,256]{1,0:T(1,128)} %refs_0_.2, s32[1,256]{1,0:T(1,128)} %param.10, s32[1,256]{1,0:T(1,128)} %refs_1_.1, s32[1,256]{1,0:T(1,128)} %refs_1_.1, s32[1,256]{1,0:T(1,128)} %refs_1_.1, s32[1,256]{1,0:T(1,128)} %refs_1_.1, s32[1,256]{1,0:T(1,128)} %refs_1_.1, s32[1,256]{1,0:T(1,128)} %refs_1_.1), dimensions={0} | concatenate | bytes 16384 | tf_op jit(solution)/shard_map/concatenate | solution.py:332
  5.5 0.1 collective-permute-done
  6.9 5.4 %collective-permute-start.1 = (f32[1,1]{1,0:T(1,128)}, f32[1,1]{1,0:T(1,128)}, u32[]{:S(2)}, u32[]{:S(2)}) collective-permute-start(f32[1,1]{1,0:T(1,128)} %add.9), channel_id=1, source_target_pairs={{0,64},{32,96},{64,0},{96,32},{1,65},{33,97},{65,1},{97,33},{2,66}... | collective-permute-start | bytes 20 | tf_op jit(solution)/shard_map/ppermute | solution.py:318
  12.2 0.2 collective-permute-done.1
  13.1 0.9 %collective-permute-start.2 = (f32[1,1]{1,0:T(1,128)}, f32[1,1]{1,0:T(1,128)}, u32[]{:S(2)}, u32[]{:S(2)}) collective-permute-start(f32[1,1]{1,0:T(1,128)} %add.10), channel_id=1, source_target_pairs={{0,16},{16,0},{1,17},{17,1},{2,18},{18,2},{3,19},{19,3},{4,20},{20... | collective-permute-start | bytes 20 | tf_op jit(solution)/shard_map/ppermute | solution.py:318
  14.0 0.3 collective-permute-done.2
  14.9 11.0 %pack.1 = (f32[16,440,128]{2,1,0:T(8,128)}, f32[16,80,128]{2,1,0:T(8,128)S(1)}) custom-call(s32[1,256]{1,0:T(1,128)} %refs_0_.2, s32[1,256]{1,0:T(1,128)} %refs_1_.1, s32[8,256]{1,0:T(8,128)} %concatenate.3.refs_2_, f32[1,1]{1,0:T(1,128)S(6)} %add.11.refs_3_, f32[8192,128]{1,0:T(8,128)} %bitcast.16, f32[8192,128]{1,0:T(8,128)} %bitcast.17), custom_call_target="tpu_custom_call" | custom-call | tf_op jit(solution)/shard_map/pack/pallas_call | solution.py:160
  25.9 51.9 %all_to_all.13 = f32[16,440,128]{2,1,0:T(8,128)S(1)} all-to-all(f32[16,440,128]{2,1,0:T(8,128)} %get-tuple-element.15), channel_id=1, replica_groups=mesh['gx_0'=4,'gx_1'=2,'gy_0'=4,'gy_1'=4] {'gy_0','gy_1'}, dimensions={0} | all-to-all | bytes 7208960 | tf_op jit(solution)/shard_map/all_to_all | solution.py:342
  77.8 0.0 copy-start
  77.8 1.8 %copy-done = f32[16,440,128]{2,1,0:T(8,128)} copy-done((f32[16,440,128]{2,1,0:T(8,128)}, f32[16,440,128]{2,1,0:T(8,128)S(1)}, u32[]{:S(2)}) %copy-start) | copy-done | bytes 3604504
  79.6 0.6 slice_reduce_fusion
  80.8 7.9 %conditional.1 = ((f32[8192,128]{1,0:T(8,128)}, f32[16,16]{1,0:T(8,128)}, f32[16,16]{1,0:T(8,128)})) conditional(s32[]{:T(128)} %convert_element_type.7, (f32[16,80,128]{2,1,0:T(8,128)S(1)}, f32[16,440,128]{2,1,0:T(8,128)}) %tuple.20, f32[16,440,128]{2,1,0:T(8,128)} %copy-done), branch_computations={%region_2.0_spmd, %region_3.0_spmd} | conditional | bytes 1310728 | solution.py:352
  80.8 7.8 %score.3 = (f32[8192,128]{1,0:T(8,128)}, f32[16,16]{1,0:T(8,128)}, f32[16,16]{1,0:T(8,128)}) custom-call(f32[16,440,128]{2,1,0:T(8,128)} %refs_0_.1), custom_call_target="tpu_custom_call" | custom-call | tf_op jit(solution)/shard_map/cond/branch_1_fun/score/pallas_call | solution.py:291
Async XLA Ops:
  1.9 3.7 %collective-permute-start = (f32[1,1]{1,0:T(1,128)}, f32[1,1]{1,0:T(1,128)}, u32[]{:S(2)}, u32[]{:S(2)}) collective-permute-start(f32[1,1]{1,0:T(1,128)} %bitcast), channel_id=1, source_target_pairs={{0,32},{32,0},{64,96},{96,64},{1,33},{33,1},{65,97},{97,65},{2,34}... | collective-permute-start | bytes 20 | tf_op jit(solution)/shard_map/ppermute | solution.py:318
  6.9 5.6 %collective-permute-start.1 = (f32[1,1]{1,0:T(1,128)}, f32[1,1]{1,0:T(1,128)}, u32[]{:S(2)}, u32[]{:S(2)}) collective-permute-start(f32[1,1]{1,0:T(1,128)} %add.9), channel_id=1, source_target_pairs={{0,64},{32,96},{64,0},{96,32},{1,65},{33,97},{65,1},{97,33},{2,66}... | collective-permute-start | bytes 20 | tf_op jit(solution)/shard_map/ppermute | solution.py:318
  13.1 1.2 %collective-permute-start.2 = (f32[1,1]{1,0:T(1,128)}, f32[1,1]{1,0:T(1,128)}, u32[]{:S(2)}, u32[]{:S(2)}) collective-permute-start(f32[1,1]{1,0:T(1,128)} %add.10), channel_id=1, source_target_pairs={{0,16},{16,0},{1,17},{17,1},{2,18},{18,2},{3,19},{19,3},{4,20},{20... | collective-permute-start | bytes 20 | tf_op jit(solution)/shard_map/ppermute | solution.py:318
  77.8 1.8 %copy-start = (f32[16,440,128]{2,1,0:T(8,128)}, f32[16,440,128]{2,1,0:T(8,128)S(1)}, u32[]{:S(2)}) copy-start(f32[16,440,128]{2,1,0:T(8,128)S(1)} %all_to_all.13) | copy-start | bytes 10813444

commit v2 on v0

v2 whole, which is shorter than its diff:
```python
import jax
import jax.numpy as jnp
from jax import lax
from jax.experimental import pallas as pl
from jax.experimental.pallas import tpu as pltpu
from jax.sharding import Mesh
from jax.sharding import PartitionSpec as P

GX_GY = ("gx_0", "gx_1", "gy_0", "gy_1")
GY = ("gy_0", "gy_1")
GX = ("gx_0", "gx_1")

KL = 0.1
LANES = 128
META = 8
FAST = 432


def lane_rows(x, rows, width):
    return (
        x.reshape(rows // 8, 8, width // LANES, LANES)
        .transpose(0, 2, 1, 3)
        .reshape(rows * width // LANES, LANES)
    )


def sliced_position(cols):
    row = lax.broadcasted_iota(jnp.int32, (cols, LANES), 0)
    return row * LANES + lax.broadcasted_iota(jnp.int32, (cols, LANES), 1)


STEPS = 8


def token_kernel(len_ref, policy_hbm, anchor_hbm, u_ref, p_ref, q_ref, policy, anchor, sem):
    slots, width = policy.shape
    rows = slots // STEPS

    def loads(step):
        part = pl.ds(pl.multiple_of(step * rows, rows), rows)
        return (
            pltpu.make_async_copy(policy_hbm.at[part], policy.at[part], sem.at[0, step]),
            pltpu.make_async_copy(anchor_hbm.at[part], anchor.at[part], sem.at[1, step]),
        )

    for step in range(STEPS):
        for load in loads(step):
            load.start()
    lane = lax.broadcasted_iota(jnp.int32, (8, LANES), 1)
    sub = lax.broadcasted_iota(jnp.int32, (8, LANES), 0)

    @pl.loop(0, STEPS)
    def _(step):
        for load in loads(step):
            load.wait()

        @pl.loop(0, rows // 8)
        def _(group):
            first = pl.multiple_of(step * rows + group * 8, 8)
            length = jnp.full((8, LANES), len_ref[0, first], jnp.int32)
            for i in range(1, 8):
                length = jnp.where(sub == i, len_ref[0, first + i], length)
            behind = lane - length
            sums_p = [jnp.zeros((8, LANES), jnp.float32)] * 4
            sums_q = [jnp.zeros((8, LANES), jnp.float32)] * 4
            for c in range(width // LANES):
                at = (pl.ds(first, 8), pl.ds(c * LANES, LANES))
                a = policy[at]
                d = anchor[at] - a
                valid = behind < -c * LANES
                u = jnp.where(valid, jnp.exp(d) - 1.0, 0.0)
                u_ref[at] = u
                sums_q[c % 4] = sums_q[c % 4] + (u - jnp.where(valid, d, 0.0))
                sums_p[c % 4] = sums_p[c % 4] + jnp.where(valid, a, 0.0)
            p_ref[pl.ds(first, 8), :] = (sums_p[0] + sums_p[1]) + (sums_p[2] + sums_p[3])
            q_ref[pl.ds(first, 8), :] = (sums_q[0] + sums_q[1]) + (sums_q[2] + sums_q[3])


def token_terms(lengths, policy, anchor):
    slots, width = policy.shape
    vmem = pl.BlockSpec(memory_space=pltpu.VMEM)
    hbm = pl.BlockSpec(memory_space=pltpu.HBM)
    small = jax.ShapeDtypeStruct((slots, LANES), jnp.float32)
    return pl.pallas_call(
        token_kernel,
        out_shape=(jax.ShapeDtypeStruct((slots, width), jnp.float32), small, small),
        in_specs=[pl.BlockSpec(memory_space=pltpu.SMEM), hbm, hbm],
        out_specs=(vmem, vmem, vmem),
        scratch_shapes=[
            pltpu.VMEM((slots, width), jnp.float32),
            pltpu.VMEM((slots, width), jnp.float32),
            pltpu.SemaphoreType.DMA((2, STEPS)),
        ],
        compiler_params=pltpu.CompilerParams(vmem_limit_bytes=24 << 20),
        cost_estimate=pl.CostEstimate(
            flops=40_000_000, bytes_accessed=12 * slots * width, transcendentals=slots * width
        ),
        name="token_terms",
    )(lengths, policy, anchor)


def pack_kernel(
    dests,
    per_dest,
    cols,
    len_ref,
    reward_ref,
    prompt_ref,
    tok_refs,
    u_ref,
    p_ref,
    q_ref,
    main,
    stage,
    sorted_p,
    sorted_q,
    slot_of,
):
    slots = dests * per_dest
    chunk = META + FAST

    def invert(s, carry):
        slot_of[prompt_ref[0, s] & (slots - 1)] = s
        return carry

    lax.fori_loop(0, slots, invert, 0, unroll=16)
    lane = lax.broadcasted_iota(jnp.int32, (8, LANES), 1)
    sub = lax.broadcasted_iota(jnp.int32, (8, LANES), 0)

    def one_dest(dest, most, ref, base):
        at = base + META
        meta = jnp.zeros((8, LANES), jnp.float32)
        for r in range(per_dest):
            p = dest * per_dest + r
            s = slot_of[p]
            length = len_ref[0, s]
            first = (s >> 3) * (8 * cols) + (s & 7)
            ref[pl.ds(at, cols), :] = u_ref[pl.ds(first, cols, stride=8), :]
            sorted_p[pl.ds(p, 1), :] = p_ref[pl.ds(s, 1), :]
            sorted_q[pl.ds(p, 1), :] = q_ref[pl.ds(s, 1), :]
            both = jnp.where(
                sub == 0,
                length.astype(jnp.float32),
                reward_ref[0, s].astype(jnp.float32) * 0.25,
            )
            meta = jnp.where(lane == r, both, meta)
            at = at + ((length + (LANES - 1)) >> 7)
        ref[pl.ds(base, META), :] = meta
        return jnp.maximum(most, at - base - META)

    last = dests - 1

    def in_place(dest, most):
        return one_dest(dest, most, main, pl.multiple_of(dest * chunk, 8))

    most = lax.fori_loop(0, last, in_place, jnp.int32(0))
    most = one_dest(last, most, stage, 0)
    main[last * chunk : (last + 1) * chunk, :] = stage[0:chunk, :]

    ones = jnp.full((8, LANES), 1.0, jnp.float32)

    def lanes(part):
        return lax.dot_general(
            ones,
            part[...],
            (((1,), (1,)), ((), ())),
            precision=lax.Precision.HIGHEST,
            preferred_element_type=jnp.float32,
        )

    sums_p, sums_q = lanes(sorted_p), lanes(sorted_q)
    tokens = jnp.sum(sum(t[...] for t in tok_refs).astype(jnp.float32), axis=1, keepdims=True)
    fill = most.astype(jnp.float32)
    for dest in range(dests):
        half = dest * per_dest // LANES * LANES
        head = slice(dest * chunk, dest * chunk + META)
        rows = jnp.where(sub == 2, sums_p[:, half : half + LANES], main[head, :])
        rows = jnp.where(sub == 3, sums_q[:, half : half + LANES], rows)
        rows = jnp.where(sub == 4, tokens, rows)
        main[head, :] = jnp.where(sub == 5, fill, rows)


def pack(lengths, rewards, prompts, tokens, u, sums_p, sums_q, dests):
    slots = lengths.shape[1]
    per_dest = slots // dests
    cols = u.shape[0] // slots
    chunk = META + FAST
    smem = pl.BlockSpec(memory_space=pltpu.SMEM)
    vmem = pl.BlockSpec(memory_space=pltpu.VMEM)

    def body(*refs):
        mine, refs = refs[:3], refs[3:]
        tok_refs, refs = refs[: len(tokens)], refs[len(tokens) :]
        pack_kernel(dests, per_dest, cols, *mine, tok_refs, *refs)

    return pl.pallas_call(
        body,
        out_shape=jax.ShapeDtypeStruct((dests * chunk, LANES), jnp.float32),
        in_specs=[smem] * 3 + [vmem] * (len(tokens) + 3),
        out_specs=vmem,
        scratch_shapes=[
            pltpu.VMEM((META + (per_dest + 1) * cols, LANES), jnp.float32),
            pltpu.VMEM((slots, LANES), jnp.float32),
            pltpu.VMEM((slots, LANES), jnp.float32),
            pltpu.SMEM((slots,), jnp.int32),
        ],
        compiler_params=pltpu.CompilerParams(vmem_limit_bytes=24 << 20),
        name="pack",
    )(lengths, rewards, prompts, *tokens, u, sums_p, sums_q).reshape(dests, chunk, LANES)


def pack_rest(lengths, prompts, u, dests):
    slots = lengths.shape[1]
    per_dest = slots // dests
    cols = u.shape[0] // slots
    spare = per_dest * cols - FAST

    def body(len_ref, prompt_ref, u_ref, rest_hbm, stage, slot_of, sem):
        def invert(s, carry):
            slot_of[prompt_ref[0, s] & (slots - 1)] = s
            return carry

        lax.fori_loop(0, slots, invert, 0)

        def one_dest(dest, carry):
            def row(r, at):
                s = slot_of[dest * per_dest + r]
                first = (s >> 3) * (8 * cols) + (s & 7)
                stage[pl.ds(at, cols), :] = u_ref[pl.ds(first, cols, stride=8), :]
                return at + ((len_ref[0, s] + (LANES - 1)) >> 7)

            lax.fori_loop(0, per_dest, row, jnp.int32(0))
            copy = pltpu.make_async_copy(stage.at[pl.ds(FAST, spare)], rest_hbm.at[dest], sem)
            copy.start()
            copy.wait()
            return carry

        lax.fori_loop(0, dests, one_dest, 0)

    smem = pl.BlockSpec(memory_space=pltpu.SMEM)
    return pl.pallas_call(
        body,
        out_shape=jax.ShapeDtypeStruct((dests, spare, LANES), jnp.float32),
        in_specs=[smem, smem, pl.BlockSpec(memory_space=pltpu.VMEM)],
        out_specs=pl.BlockSpec(memory_space=pl.ANY),
        scratch_shapes=[
            pltpu.VMEM(((per_dest + 1) * cols, LANES), jnp.float32),
            pltpu.SMEM((slots,), jnp.int32),
            pltpu.SemaphoreType.DMA,
        ],
        compiler_params=pltpu.CompilerParams(vmem_limit_bytes=16 << 20),
        name="pack_rest",
    )(lengths, prompts, u)


def score_kernel(members, per_dest, cols, scales, refs):
    main, grad_hbm, loss_ref, adv_ref, table_ref, more_ref, tail, grad, numbers, num_sem, out_sem = refs
    grad_scale, loss_scale = scales
    width = per_dest * cols
    chunk = META + FAST

    def field(i):
        return jnp.concatenate(
            [main[k * chunk + i : k * chunk + i + 1, :] for k in range(members)], axis=0
        )

    reward = field(1)
    total = jnp.sum(reward, axis=0, keepdims=True)
    advantage = (members * reward - total) / (members - 1)
    tokens = jnp.sum(field(4), axis=0, keepdims=True)
    scale = grad_scale / tokens
    table_ref[0] = field(0)
    table_ref[1] = -advantage * scale
    table_ref[2] = jnp.broadcast_to(scale * -KL, (members, LANES))
    to_scalars = pltpu.make_async_copy(table_ref, numbers, num_sem)
    to_scalars.start()

    start = lax.rem(lax.axis_index(GY) * per_dest, LANES)
    shift = lax.rem(LANES - start, LANES)
    sums_p = pltpu.roll(field(2), shift, 1)
    sums_q = pltpu.roll(field(3), shift, 1)
    loss = (KL * sums_q - advantage * sums_p) * (loss_scale / tokens)
    loss_ref[...] = loss[:, 0:per_dest]
    adv_ref[...] = advantage[:, 0:per_dest]
    most = jnp.max(field(5), axis=0, keepdims=True)
    more_ref[...] = jnp.where(most > FAST, 1, 0)
    position = sliced_position(cols)
    last = members - 1
    tail[0:chunk, :] = main[last * chunk : (last + 1) * chunk, :]
    to_scalars.wait()

    def out_copy(k):
        part = pl.ds(pl.multiple_of(k * width, width), width)
        return pltpu.make_async_copy(grad.at[part], grad_hbm.at[part], out_sem.at[k])

    def one_member(k, ref, base):
        slope = numbers[2, 0, 0]
        at = base + META
        for r in range(per_dest):
            length = numbers[0, k, r].astype(jnp.int32)
            u = ref[pl.ds(at, cols), :]
            y = jnp.where(position < length, numbers[1, k, r] + slope * u, 0.0)
            first = k * width + r // 8 * (8 * cols) + r % 8
            grad[pl.ds(first, cols, stride=8), :] = y
            at = jnp.minimum(at + ((length + (LANES - 1)) >> 7), base + chunk)
        out_copy(k).start()

    @pl.loop(0, last)
    def _(k):
        one_member(k, main, pl.multiple_of(k * chunk, 8))

    one_member(last, tail, 0)

    @pl.loop(0, members)
    def _(k):
        out_copy(k).wait()


def score(main, scales, per_dest, cols):
    members, chunk, _ = main.shape
    full = per_dest * cols
    hbm = pl.BlockSpec(memory_space=pl.ANY)
    vmem = pl.BlockSpec(memory_space=pltpu.VMEM)

    def body(*refs):
        score_kernel(members, per_dest, cols, scales, refs)

    small = jax.ShapeDtypeStruct((members, per_dest), jnp.float32)
    return pl.pallas_call(
        body,
        out_shape=(
            jax.ShapeDtypeStruct((members * full, LANES), jnp.float32),
            small,
            small,
            jax.ShapeDtypeStruct((3, members, LANES), jnp.float32),
            jax.ShapeDtypeStruct((1, LANES), jnp.int32),
        ),
        in_specs=[vmem],
        out_specs=(hbm, vmem, vmem, vmem, vmem),
        scratch_shapes=[
            pltpu.VMEM((chunk + cols, LANES), jnp.float32),
            pltpu.VMEM((members * full, LANES), jnp.float32),
            pltpu.SMEM((3, members, LANES), jnp.float32),
            pltpu.SemaphoreType.DMA,
            pltpu.SemaphoreType.DMA((members,)),
        ],
        compiler_params=pltpu.CompilerParams(vmem_limit_bytes=24 << 20),
        name="score",
    )(main.reshape(members * chunk, LANES))


def finish_kernel(members, per_dest, cols, refs):
    table_hbm, rest_hbm, _, grad_hbm, numbers, rest, grad, sem = refs
    width = per_dest * cols
    spare = width - FAST
    load = pltpu.make_async_copy(table_hbm, numbers, sem.at[0])
    load.start()
    load.wait()
    position = sliced_position(cols)
    row_of = lax.broadcasted_iota(jnp.int32, (cols, LANES), 0)

    @pl.loop(0, members)
    def _(k):
        place = grad_hbm.at[pl.ds(k * width, width)]
        loads = (
            pltpu.make_async_copy(rest_hbm.at[k], rest.at[pl.ds(cols, spare)], sem.at[0]),
            pltpu.make_async_copy(place, grad, sem.at[1]),
        )
        for load in loads:
            load.start()
        for load in loads:
            load.wait()

        def row(r, at):
            length = numbers[0, k, r].astype(jnp.int32)
            end = at + ((length + (LANES - 1)) >> 7)

            @pl.when(end > FAST)
            def _():
                u = rest[pl.ds(at - FAST + cols, cols), :]
                y = jnp.where(position < length, numbers[1, k, r] + numbers[2, 0, 0] * u, 0.0)
                first = (r >> 3) * (8 * cols) + (r & 7)
                old = grad[pl.ds(first, cols, stride=8), :]
                grad[pl.ds(first, cols, stride=8), :] = jnp.where(row_of + at >= FAST, y, old)

            return end

        lax.fori_loop(0, per_dest, row, jnp.int32(0))
        store = pltpu.make_async_copy(grad, place, sem.at[1])
        store.start()
        store.wait()


def finish(grad, rest, table, per_dest, cols):
    members = rest.shape[0]
    full = per_dest * cols
    hbm = pl.BlockSpec(memory_space=pl.ANY)

    def body(*refs):
        finish_kernel(members, per_dest, cols, refs)

    return pl.pallas_call(
        body,
        out_shape=jax.ShapeDtypeStruct(grad.shape, jnp.float32),
        in_specs=[hbm, hbm, hbm],
        out_specs=hbm,
        input_output_aliases={2: 0},
        scratch_shapes=[
            pltpu.SMEM((3, members, LANES), jnp.float32),
            pltpu.VMEM((full - FAST + 2 * cols, LANES), jnp.float32),
            pltpu.VMEM((full, LANES), jnp.float32),
            pltpu.SemaphoreType.DMA((2,)),
        ],
        compiler_params=pltpu.CompilerParams(vmem_limit_bytes=8 << 20),
        name="finish",
    )(table, rest, grad)


def peers(x, axis):
    size = lax.axis_size(axis)
    return [
        lax.ppermute(x, axis, [(i, (i + step) % size) for i in range(size)])
        for step in range(1, size)
    ]


def body(policy_logp, anchor_logp, lengths, rewards, slot_prompt):
    members_dev, slots, seq_slots = policy_logp.shape
    dests = lax.axis_size(GY)
    per_dest = slots // dests
    cols = seq_slots // LANES
    members = members_dev * dests
    samples = members * slots * lax.axis_size(GX)
    scales = (float(samples * seq_slots), float(samples))
    tokens = [lengths] + peers(lengths, GX)
    u, sums_p, sums_q = token_terms(
        lengths,
        pltpu.with_memory_space_constraint(policy_logp[0], pltpu.HBM),
        pltpu.with_memory_space_constraint(anchor_logp[0], pltpu.HBM),
    )
    u = lane_rows(u, slots, seq_slots)
    main = pack(lengths, rewards, slot_prompt, tokens, u, sums_p, sums_q, dests)
    main = lax.all_to_all(main, GY, 0, 0, tiled=True)
    grad, loss, advantage, table, more = score(main, scales, per_dest, cols)

    def the_rest(state):
        grad, _ = state
        rest = pack_rest(lengths, slot_prompt, u, dests)
        got = lax.all_to_all(rest, GY, 0, 0, tiled=True)
        return finish(grad, got, table, per_dest, cols), jnp.int32(0)

    grad, _ = lax.while_loop(lambda state: state[1] > 0, the_rest, (grad, more[0, 0]))
    grad = (
        grad.reshape(members, per_dest // 8, cols, 8, LANES)
        .transpose(0, 1, 3, 2, 4)
        .reshape(members, per_dest, seq_slots)
    )
    return grad, loss, advantage


def solution(mesh):
    torus = Mesh(mesh.devices.reshape(4, 2, 4, 4), ("gx_0", "gx_1", "gy_0", "gy_1"))
    return jax.shard_map(
        body,
        mesh=torus,
        in_specs=(P(GY, GX, None), P(GY, GX, None), P(GY, GX), P(GY, GX), P(GY, GX)),
        out_specs=(P(None, GX_GY, None), P(None, GX_GY), P(None, GX_GY)),
        check_vma=False,
    )
```

time: 138 us -> 75.7 us (0.55)
  blocking collectives: 89.3 us -> 52 us
  local copies, waits for them, and re-layouts: 37.2 us -> 0.02 us
  Pallas kernels: 0 us -> 12.5 us
  starting transfers between devices: 0 us -> 9.68 us
  other arithmetic: 8.42 us -> 0 us
    psum x4 -> x0, blocking collectives: 38 us -> none  [by_axis(): x = lax.psum(x, axis)]
    gather x4 -> x0, local copies, waits for them, and re-layouts: 19.6 us -> none  [the longest x1 7.89 us: body(): jnp.take_along_axis(policy_logp, inverse[:, :, None], axis=1)]
    pallas_call x0 -> x3, Pallas kernels: none -> 12.5 us  [the longest x1 4.57 us: token_terms(): pl.pallas_call(token_kernel, out_shape=(jax.ShapeDtypeStruct((slots, widt...]
    concatenate x3 -> x0, local copies, waits for them, and re-layouts: 12.2 us -> none  [the longest x2 12.2 us: sent_together(): both = jnp.concatenate(columns, axis=along)]
    ppermute x0 -> x7, starting transfers between devices: none -> 9.68 us  [peers(): lax.ppermute(x, axis, [(i, (i + step) % size) for i in range(size)])]
    reduce_sum x2 -> x0, other arithmetic: 7.65 us -> none  [the longest x1 6.36 us: score_tokens(): jnp.sum(jnp.where(valid, token_term, 0.0), axis=2) * loss_scale]
    slice x2 -> x0, local copies, waits for them, and re-layouts: 3.33 us -> none  [sent_together(): piece = out[..., at:at + column.shape[along]]]
    scatter x1 -> x0, local copies, waits for them, and re-layouts: 1.4 us -> none  [body(): jnp.zeros((members_dev, slots), jnp.int32).at[member_rows, local_prompt]]
  transfers between devices with their start and end apart: 0 -> 7, of which waited for: 0 -> 0; matrix products, arithmetic and copies ran while one was open for 0% -> 0% of each run, Pallas kernels for 0% -> 6%
where the time goes in v2:
time: 75.7 us; the launch traced here: 75.5 us
  blocking collectives  52 us (69%)
  Pallas kernels  12.5 us (17%)
  starting transfers between devices  9.68 us (13%)
    all_to_all x1, blocking collectives, body(): main = lax.all_to_all(main, GY, 0, 0, tiled=True)  52 us
    ppermute x7, starting transfers between devices, peers(): lax.ppermute(x, axis, [(i, (i + step) % size) for i in range(size)])  9.68 us
    pallas_call x1, Pallas kernels, token_terms(): pl.pallas_call(token_kernel, out_shape=(jax.ShapeDtypeStruct((slots, widt...  4.57 us
    pallas_call x1, Pallas kernels, pack(): pl.pallas_call(body, out_shape=jax.ShapeDtypeStruct((dests * chunk, LANES...  4.08 us
    pallas_call x1, Pallas kernels, score(): pl.pallas_call(body, out_shape=(jax.ShapeDtypeStruct((members * full, LAN...  3.81 us
  transfers between devices with their start and end apart: 7, of which 0 were waited for; matrix products, arithmetic and copies ran while one was open for 0% of the time, Pallas kernels for 6%

profile of v2, /device:TPU:0, one launch (start us, length us, event | category | flops | bytes accessed | tf_op | source)
XLA Modules:
  0.0 75.5 jit_solution(10588484009852733256)
XLA Ops:
  0.6 0.0 collective-permute-start
  0.7 2.1 %collective-permute-start.1 = (s32[1,256]{1,0:T(1,128)}, s32[1,256]{1,0:T(1,128)S(1)}, u32[]{:S(2)}, u32[]{:S(2)}) collective-permute-start(s32[1,256]{1,0:T(1,128)} %refs_3_.1), channel_id=1, source_target_pairs={{0,32},{16,48},{32,64},{48,80},{64,96},{80,112},{96,0},{112,16},{1... | collective-permute-start | bytes 3080 | tf_op jit(solution)/shard_map/ppermute | solution.py:422
  2.8 2.9 %collective-permute-start.2 = (s32[1,256]{1,0:T(1,128)}, s32[1,256]{1,0:T(1,128)S(1)}, u32[]{:S(2)}, u32[]{:S(2)}) collective-permute-start(s32[1,256]{1,0:T(1,128)} %refs_3_.1), channel_id=1, source_target_pairs={{0,48},{16,64},{32,80},{48,96},{64,112},{80,0},{96,16},{112,32},{1... | collective-permute-start | bytes 3080 | tf_op jit(solution)/shard_map/ppermute | solution.py:422
  5.7 1.2 %collective-permute-start.3 = (s32[1,256]{1,0:T(1,128)}, s32[1,256]{1,0:T(1,128)S(1)}, u32[]{:S(2)}, u32[]{:S(2)}) collective-permute-start(s32[1,256]{1,0:T(1,128)} %refs_3_.1), channel_id=1, source_target_pairs={{0,64},{16,80},{32,96},{48,112},{64,0},{80,16},{96,32},{112,48},{1... | collective-permute-start | bytes 3080 | tf_op jit(solution)/shard_map/ppermute | solution.py:422
  6.8 2.5 %collective-permute-start.4 = (s32[1,256]{1,0:T(1,128)}, s32[1,256]{1,0:T(1,128)S(1)}, u32[]{:S(2)}, u32[]{:S(2)}) collective-permute-start(s32[1,256]{1,0:T(1,128)} %refs_3_.1), channel_id=1, source_target_pairs={{0,80},{16,96},{32,112},{48,0},{64,16},{80,32},{96,48},{112,64},{1... | collective-permute-start | bytes 3080 | tf_op jit(solution)/shard_map/ppermute | solution.py:422
  9.3 0.0 collective-permute-done.refs_4_
  9.3 1.0 %collective-permute-start.5 = (s32[1,256]{1,0:T(1,128)}, s32[1,256]{1,0:T(1,128)S(1)}, u32[]{:S(2)}, u32[]{:S(2)}) collective-permute-start(s32[1,256]{1,0:T(1,128)} %refs_3_.1), channel_id=1, source_target_pairs={{0,96},{16,112},{32,0},{48,16},{64,32},{80,48},{96,64},{112,80},{1... | collective-permute-start | bytes 3080 | tf_op jit(solution)/shard_map/ppermute | solution.py:422
  10.3 0.0 collective-permute-done.1.refs_5_
  10.3 0.0 collective-permute-start.6
  10.3 0.0 copy-start
  10.3 0.0 copy-start.2
  10.3 0.0 copy-start.3
  10.4 4.6 %token_terms.1 = (f32[256,4096]{1,0:T(8,128)S(1)}, f32[256,128]{1,0:T(8,128)S(1)}, f32[256,128]{1,0:T(8,128)S(1)}) custom-call(s32[1,256]{1,0:T(1,128)} %refs_3_.1, f32[256,4096]{1,0:T(8,128)} %bitcast.21, f32[256,4096]{1,0:T(8,128)} %bitcast.22), custom_call_target="tpu_custom_call" | custom-call | flops 40000000 | bytes 12582912 | tf_op jit(solution)/shard_map/token_terms/pallas_call | solution.py:84
  14.9 0.0 copy-start.1
  14.9 0.0 collective-permute-done.2.refs_6_
  15.0 0.0 collective-permute-done.3.refs_7_
  15.0 0.0 collective-permute-done.4.refs_8_
  15.0 0.0 collective-permute-done.5.refs_9_
  15.0 0.0 collective-permute-done.6.refs_10_
  15.0 0.0 copy-done
  15.0 0.0 copy-done.2
  15.0 0.0 copy-done.3
  15.0 4.1 %pack.1 = f32[7040,128]{1,0:T(8,128)S(1)} custom-call(s32[1,256]{1,0:T(1,128)S(1)} %copy-done.2, s32[1,256]{1,0:T(1,128)S(1)} %copy-done, s32[1,256]{1,0:T(1,128)S(1)} %copy-done.3, s32[1,256]{1,0:T(1,128)S(1)} %copy-done.2, s32[1,256]{1,0:T(1,128)S(1)} %collective-permute-done.refs_4_, s32[1,256]{1,0:T(1,128)S(1)} %collective-permute-done.1.refs_5_, ...), custom_call_target="tpu_custom_call" | custom-call | tf_op jit(solution)/shard_map/pack/pallas_call | solution.py:196
  19.1 52.0 %all_to_all.9 = f32[16,440,128]{2,1,0:T(8,128)S(1)} all-to-all(f32[16,440,128]{2,1,0:T(8,128)S(1)} %bitcast.17), channel_id=1, replica_groups=mesh['gx_0'=4,'gx_1'=2,'gy_0'=4,'gy_1'=4] {'gy_0','gy_1'}, dimensions={0} | all-to-all | bytes 7208960 | tf_op jit(solution)/shard_map/all_to_all | solution.py:443
  71.1 0.0 copy-done.1
  71.1 3.8 %score.1 = (f32[8192,128]{1,0:T(8,128)}, f32[16,16]{1,0:T(8,128)}, f32[16,16]{1,0:T(8,128)}, f32[3,16,128]{2,1,0:T(8,128)S(1)}, s32[1,128]{1,0:T(1,128)}) custom-call(f32[7040,128]{1,0:T(8,128)S(1)} %bitcast.16), custom_call_target="tpu_custom_call" | custom-call | tf_op jit(solution)/shard_map/score/pallas_call | solution.py:329
  74.9 0.6 while.9
Async XLA Ops:
  0.6 8.7 %collective-permute-start = (s32[1,256]{1,0:T(1,128)}, s32[1,256]{1,0:T(1,128)S(1)}, u32[]{:S(2)}, u32[]{:S(2)}) collective-permute-start(s32[1,256]{1,0:T(1,128)} %refs_3_.1), channel_id=1, source_target_pairs={{0,16},{16,32},{32,48},{48,64},{64,80},{80,96},{96,112},{112,0},{1... | collective-permute-start | bytes 3080 | tf_op jit(solution)/shard_map/ppermute | solution.py:422
  0.7 9.7 %collective-permute-start.1 = (s32[1,256]{1,0:T(1,128)}, s32[1,256]{1,0:T(1,128)S(1)}, u32[]{:S(2)}, u32[]{:S(2)}) collective-permute-start(s32[1,256]{1,0:T(1,128)} %refs_3_.1), channel_id=1, source_target_pairs={{0,32},{16,48},{32,64},{48,80},{64,96},{80,112},{96,0},{112,16},{1... | collective-permute-start | bytes 3080 | tf_op jit(solution)/shard_map/ppermute | solution.py:422
  2.8 12.2 %collective-permute-start.2 = (s32[1,256]{1,0:T(1,128)}, s32[1,256]{1,0:T(1,128)S(1)}, u32[]{:S(2)}, u32[]{:S(2)}) collective-permute-start(s32[1,256]{1,0:T(1,128)} %refs_3_.1), channel_id=1, source_target_pairs={{0,48},{16,64},{32,80},{48,96},{64,112},{80,0},{96,16},{112,32},{1... | collective-permute-start | bytes 3080 | tf_op jit(solution)/shard_map/ppermute | solution.py:422
  5.7 9.3 %collective-permute-start.3 = (s32[1,256]{1,0:T(1,128)}, s32[1,256]{1,0:T(1,128)S(1)}, u32[]{:S(2)}, u32[]{:S(2)}) collective-permute-start(s32[1,256]{1,0:T(1,128)} %refs_3_.1), channel_id=1, source_target_pairs={{0,64},{16,80},{32,96},{48,112},{64,0},{80,16},{96,32},{112,48},{1... | collective-permute-start | bytes 3080 | tf_op jit(solution)/shard_map/ppermute | solution.py:422
  6.8 8.2 %collective-permute-start.4 = (s32[1,256]{1,0:T(1,128)}, s32[1,256]{1,0:T(1,128)S(1)}, u32[]{:S(2)}, u32[]{:S(2)}) collective-permute-start(s32[1,256]{1,0:T(1,128)} %refs_3_.1), channel_id=1, source_target_pairs={{0,80},{16,96},{32,112},{48,0},{64,16},{80,32},{96,48},{112,64},{1... | collective-permute-start | bytes 3080 | tf_op jit(solution)/shard_map/ppermute | solution.py:422
  9.3 5.7 %collective-permute-start.5 = (s32[1,256]{1,0:T(1,128)}, s32[1,256]{1,0:T(1,128)S(1)}, u32[]{:S(2)}, u32[]{:S(2)}) collective-permute-start(s32[1,256]{1,0:T(1,128)} %refs_3_.1), channel_id=1, source_target_pairs={{0,96},{16,112},{32,0},{48,16},{64,32},{80,48},{96,64},{112,80},{1... | collective-permute-start | bytes 3080 | tf_op jit(solution)/shard_map/ppermute | solution.py:422
  10.3 4.7 %collective-permute-start.6 = (s32[1,256]{1,0:T(1,128)}, s32[1,256]{1,0:T(1,128)S(1)}, u32[]{:S(2)}, u32[]{:S(2)}) collective-permute-start(s32[1,256]{1,0:T(1,128)} %refs_3_.1), channel_id=1, source_target_pairs={{0,112},{16,0},{32,16},{48,32},{64,48},{80,64},{96,80},{112,96},{1... | collective-permute-start | bytes 3080 | tf_op jit(solution)/shard_map/ppermute | solution.py:422
  10.3 4.7 %copy-start = (s32[1,256]{1,0:T(1,128)S(1)}, s32[1,256]{1,0:T(1,128)}, u32[]{:S(2)}) copy-start(s32[1,256]{1,0:T(1,128)} %refs_1_.1) | copy-start | bytes 3076
  10.3 4.7 %copy-start.2 = (s32[1,256]{1,0:T(1,128)S(1)}, s32[1,256]{1,0:T(1,128)}, u32[]{:S(2)}) copy-start(s32[1,256]{1,0:T(1,128)} %refs_3_.1) | copy-start | bytes 3076
  10.3 4.7 %copy-start.3 = (s32[1,256]{1,0:T(1,128)S(1)}, s32[1,256]{1,0:T(1,128)}, u32[]{:S(2)}) copy-start(s32[1,256]{1,0:T(1,128)} %refs_2_.1) | copy-start | bytes 3076
  14.9 56.2 %copy-start.1 = (f32[256,4096]{1,0:T(8,128)}, f32[256,4096]{1,0:T(8,128)S(1)}, u32[]{:S(2)}) copy-start(f32[256,4096]{1,0:T(8,128)S(1)} %get-tuple-element.42) | copy-start | bytes 12582916

commit v3 on v2

--- a/solution.py
+++ b/solution.py
@@ -29,12 +29,32 @@
     return row * LANES + lax.broadcasted_iota(jnp.int32, (cols, LANES), 1)
 
 
+SPAN = LANES // 4
+LEN, REWARD = 2 * SPAN, 3 * SPAN
 STEPS = 8
 
 
-def token_kernel(len_ref, policy_hbm, anchor_hbm, u_ref, p_ref, q_ref, policy, anchor, sem):
+def token_kernel(
+    dests,
+    small_hbm,
+    policy_hbm,
+    anchor_hbm,
+    u_ref,
+    sums_ref,
+    slot_of,
+    policy,
+    anchor,
+    parts,
+    len_ref,
+    reward_ref,
+    prompt_ref,
+    sem,
+    small_sem,
+):
     slots, width = policy.shape
     rows = slots // STEPS
+    cols = width // LANES
+    per_dest = slots // dests
 
     def loads(step):
         part = pl.ds(pl.multiple_of(step * rows, rows), rows)
@@ -43,9 +63,23 @@
             pltpu.make_async_copy(anchor_hbm.at[part], anchor.at[part], sem.at[1, step]),
         )
 
-    for step in range(STEPS):
+    small = [
+        pltpu.make_async_copy(src, dst, small_sem.at[i])
+        for i, (src, dst) in enumerate(zip(small_hbm, (prompt_ref, len_ref, reward_ref)))
+    ]
+    for load in (*loads(0), *small):
+        load.start()
+    for step in range(1, STEPS):
         for load in loads(step):
             load.start()
+    for load in small:
+        load.wait()
+
+    def invert(s, carry):
+        slot_of[0, prompt_ref[0, s] & (slots - 1)] = s
+        return carry
+
+    lax.fori_loop(0, slots, invert, 0, unroll=16)
     lane = lax.broadcasted_iota(jnp.int32, (8, LANES), 1)
     sub = lax.broadcasted_iota(jnp.int32, (8, LANES), 0)
 
@@ -58,12 +92,17 @@
         def _(group):
             first = pl.multiple_of(step * rows + group * 8, 8)
             length = jnp.full((8, LANES), len_ref[0, first], jnp.int32)
+            reward = jnp.full((8, LANES), reward_ref[0, first], jnp.int32)
             for i in range(1, 8):
                 length = jnp.where(sub == i, len_ref[0, first + i], length)
+                reward = jnp.where(sub == i, reward_ref[0, first + i], reward)
+            sums_ref[pl.ds(first, 8), :] = jnp.where(lane < LEN + SPAN, length, reward).astype(
+                jnp.float32
+            )
             behind = lane - length
             sums_p = [jnp.zeros((8, LANES), jnp.float32)] * 4
             sums_q = [jnp.zeros((8, LANES), jnp.float32)] * 4
-            for c in range(width // LANES):
+            for c in range(cols):
                 at = (pl.ds(first, 8), pl.ds(c * LANES, LANES))
                 a = policy[at]
                 d = anchor[at] - a
@@ -72,115 +111,113 @@
                 u_ref[at] = u
                 sums_q[c % 4] = sums_q[c % 4] + (u - jnp.where(valid, d, 0.0))
                 sums_p[c % 4] = sums_p[c % 4] + jnp.where(valid, a, 0.0)
-            p_ref[pl.ds(first, 8), :] = (sums_p[0] + sums_p[1]) + (sums_p[2] + sums_p[3])
-            q_ref[pl.ds(first, 8), :] = (sums_q[0] + sums_q[1]) + (sums_q[2] + sums_q[3])
-
-
-def token_terms(lengths, policy, anchor):
+            parts[0, pl.ds(first, 8), :] = (sums_p[0] + sums_p[1]) + (sums_p[2] + sums_p[3])
+            parts[1, pl.ds(first, 8), :] = (sums_q[0] + sums_q[1]) + (sums_q[2] + sums_q[3])
+
+    lane = lax.broadcasted_iota(jnp.int32, (slots, LANES), 1)
+    p, q = (
+        x + pltpu.roll(x, SPAN, 1)
+        for x in (x + pltpu.roll(x, 2 * SPAN, 1) for x in (parts[0], parts[1]))
+    )
+    rest = jnp.where(lane < 2 * SPAN, q, sums_ref[...])
+    sums_ref[...] = jnp.where(lane < SPAN, p, rest)
+
+
+def token_terms(lengths, rewards, prompts, policy, anchor, dests):
     slots, width = policy.shape
     vmem = pl.BlockSpec(memory_space=pltpu.VMEM)
-    hbm = pl.BlockSpec(memory_space=pltpu.HBM)
-    small = jax.ShapeDtypeStruct((slots, LANES), jnp.float32)
+    smem = pl.BlockSpec(memory_space=pltpu.SMEM)
+    hbm = pl.BlockSpec(memory_space=pl.ANY)
+
+    def body(*refs):
+        token_kernel(dests, refs[:3], *refs[3:])
+
     return pl.pallas_call(
-        token_kernel,
-        out_shape=(jax.ShapeDtypeStruct((slots, width), jnp.float32), small, small),
-        in_specs=[pl.BlockSpec(memory_space=pltpu.SMEM), hbm, hbm],
-        out_specs=(vmem, vmem, vmem),
+        body,
+        out_shape=(
+            jax.ShapeDtypeStruct((slots, width), jnp.float32),
+            jax.ShapeDtypeStruct((slots, LANES), jnp.float32),
+            jax.ShapeDtypeStruct((1, slots), jnp.int32),
+        ),
+        in_specs=[hbm] * 5,
+        out_specs=(vmem, vmem, smem),
         scratch_shapes=[
             pltpu.VMEM((slots, width), jnp.float32),
             pltpu.VMEM((slots, width), jnp.float32),
+            pltpu.VMEM((2, slots, LANES), jnp.float32),
+            pltpu.SMEM((1, slots), jnp.int32),
+            pltpu.SMEM((1, slots), jnp.int32),
+            pltpu.SMEM((1, slots), jnp.int32),
             pltpu.SemaphoreType.DMA((2, STEPS)),
+            pltpu.SemaphoreType.DMA((3,)),
         ],
         compiler_params=pltpu.CompilerParams(vmem_limit_bytes=24 << 20),
         cost_estimate=pl.CostEstimate(
             flops=40_000_000, bytes_accessed=12 * slots * width, transcendentals=slots * width
         ),
         name="token_terms",
-    )(lengths, policy, anchor)
+    )(prompts, lengths, rewards, policy, anchor)
 
 
 def pack_kernel(
     dests,
     per_dest,
     cols,
+    slot_of,
     len_ref,
-    reward_ref,
-    prompt_ref,
     tok_refs,
     u_ref,
-    p_ref,
-    q_ref,
+    sums_ref,
     main,
     stage,
-    sorted_p,
-    sorted_q,
-    slot_of,
+    in_order,
 ):
     slots = dests * per_dest
     chunk = META + FAST
-
-    def invert(s, carry):
-        slot_of[prompt_ref[0, s] & (slots - 1)] = s
-        return carry
-
-    lax.fori_loop(0, slots, invert, 0, unroll=16)
-    lane = lax.broadcasted_iota(jnp.int32, (8, LANES), 1)
-    sub = lax.broadcasted_iota(jnp.int32, (8, LANES), 0)
+    last = dests - 1
 
     def one_dest(dest, most, ref, base):
-        at = base + META
-        meta = jnp.zeros((8, LANES), jnp.float32)
-        for r in range(per_dest):
+        def row(r, at):
             p = dest * per_dest + r
-            s = slot_of[p]
-            length = len_ref[0, s]
+            s = slot_of[0, p]
             first = (s >> 3) * (8 * cols) + (s & 7)
             ref[pl.ds(at, cols), :] = u_ref[pl.ds(first, cols, stride=8), :]
-            sorted_p[pl.ds(p, 1), :] = p_ref[pl.ds(s, 1), :]
-            sorted_q[pl.ds(p, 1), :] = q_ref[pl.ds(s, 1), :]
-            both = jnp.where(
-                sub == 0,
-                length.astype(jnp.float32),
-                reward_ref[0, s].astype(jnp.float32) * 0.25,
-            )
-            meta = jnp.where(lane == r, both, meta)
-            at = at + ((length + (LANES - 1)) >> 7)
-        ref[pl.ds(base, META), :] = meta
-        return jnp.maximum(most, at - base - META)
-
-    last = dests - 1
+            in_order[pl.ds(p, 1), :] = sums_ref[pl.ds(s, 1), :]
+            return at + ((len_ref[0, s] + (LANES - 1)) >> 7)
+
+        end = lax.fori_loop(0, per_dest, row, base + META, unroll=4)
+        return jnp.maximum(most, end - base - META)
 
     def in_place(dest, most):
         return one_dest(dest, most, main, pl.multiple_of(dest * chunk, 8))
 
     most = lax.fori_loop(0, last, in_place, jnp.int32(0))
     most = one_dest(last, most, stage, 0)
-    main[last * chunk : (last + 1) * chunk, :] = stage[0:chunk, :]
-
-    ones = jnp.full((8, LANES), 1.0, jnp.float32)
-
-    def lanes(part):
-        return lax.dot_general(
-            ones,
-            part[...],
-            (((1,), (1,)), ((), ())),
-            precision=lax.Precision.HIGHEST,
-            preferred_element_type=jnp.float32,
-        )
-
-    sums_p, sums_q = lanes(sorted_p), lanes(sorted_q)
+    main[last * chunk + META : (last + 1) * chunk, :] = stage[META:chunk, :]
+
+    sub = lax.broadcasted_iota(jnp.int32, (8, LANES), 0)
+    lane = lax.broadcasted_iota(jnp.int32, (8, LANES), 1)
+    pick = jnp.where((sub == 0) & (lane == LEN), 1.0, 0.0)
+    pick = jnp.where((sub == 1) & (lane == REWARD), 0.25, pick)
+    pick = jnp.where((sub == 2) & (lane < SPAN), 1.0, pick)
+    pick = jnp.where((sub == 3) & (lane >= SPAN) & (lane < 2 * SPAN), 1.0, pick)
+    head = lax.dot_general(
+        pick,
+        in_order[...],
+        (((1,), (1,)), ((), ())),
+        precision=lax.Precision.HIGHEST,
+        preferred_element_type=jnp.float32,
+    )
     tokens = jnp.sum(sum(t[...] for t in tok_refs).astype(jnp.float32), axis=1, keepdims=True)
-    fill = most.astype(jnp.float32)
+    sub = lax.broadcasted_iota(jnp.int32, (8, slots), 0)
+    head = jnp.where(sub == 4, tokens, head)
+    head = jnp.where(sub == 5, most.astype(jnp.float32), head)
     for dest in range(dests):
         half = dest * per_dest // LANES * LANES
-        head = slice(dest * chunk, dest * chunk + META)
-        rows = jnp.where(sub == 2, sums_p[:, half : half + LANES], main[head, :])
-        rows = jnp.where(sub == 3, sums_q[:, half : half + LANES], rows)
-        rows = jnp.where(sub == 4, tokens, rows)
-        main[head, :] = jnp.where(sub == 5, fill, rows)
-
-
-def pack(lengths, rewards, prompts, tokens, u, sums_p, sums_q, dests):
+        main[dest * chunk : dest * chunk + META, :] = head[:, half : half + LANES]
+
+
+def pack(slot_of, lengths, tokens, u, sums, dests):
     slots = lengths.shape[1]
     per_dest = slots // dests
     cols = u.shape[0] // slots
@@ -189,42 +226,35 @@
     vmem = pl.BlockSpec(memory_space=pltpu.VMEM)
 
     def body(*refs):
-        mine, refs = refs[:3], refs[3:]
+        small, refs = refs[:2], refs[2:]
         tok_refs, refs = refs[: len(tokens)], refs[len(tokens) :]
-        pack_kernel(dests, per_dest, cols, *mine, tok_refs, *refs)
+        pack_kernel(dests, per_dest, cols, *small, tok_refs, *refs)
 
     return pl.pallas_call(
         body,
         out_shape=jax.ShapeDtypeStruct((dests * chunk, LANES), jnp.float32),
-        in_specs=[smem] * 3 + [vmem] * (len(tokens) + 3),
+        in_specs=[smem] * 2 + [vmem] * (len(tokens) + 2),
         out_specs=vmem,
         scratch_shapes=[
             pltpu.VMEM((META + (per_dest + 1) * cols, LANES), jnp.float32),
             pltpu.VMEM((slots, LANES), jnp.float32),
-            pltpu.VMEM((slots, LANES), jnp.float32),
-            pltpu.SMEM((slots,), jnp.int32),
         ],
         compiler_params=pltpu.CompilerParams(vmem_limit_bytes=24 << 20),
         name="pack",
-    )(lengths, rewards, prompts, *tokens, u, sums_p, sums_q).reshape(dests, chunk, LANES)
-
-
-def pack_rest(lengths, prompts, u, dests):
+    )(slot_of, lengths, *tokens, u, sums).reshape(dests, chunk, LANES)
+
+
+def pack_rest(slot_of, lengths, u, dests):
     slots = lengths.shape[1]
     per_dest = slots // dests
     cols = u.shape[0] // slots
     spare = per_dest * cols - FAST
 
-    def body(len_ref, prompt_ref, u_ref, rest_hbm, stage, slot_of, sem):
-        def invert(s, carry):
-            slot_of[prompt_ref[0, s] & (slots - 1)] = s
-            return carry
-
-        lax.fori_loop(0, slots, invert, 0)
-
-        def one_dest(dest, carry):
+    def body(slot_of, len_ref, u_ref, rest_hbm, stage, sem):
+        @pl.loop(0, dests)
+        def _(dest):
             def row(r, at):
-                s = slot_of[dest * per_dest + r]
+                s = slot_of[0, dest * per_dest + r]
                 first = (s >> 3) * (8 * cols) + (s & 7)
                 stage[pl.ds(at, cols), :] = u_ref[pl.ds(first, cols, stride=8), :]
                 return at + ((len_ref[0, s] + (LANES - 1)) >> 7)
@@ -233,9 +263,6 @@
             copy = pltpu.make_async_copy(stage.at[pl.ds(FAST, spare)], rest_hbm.at[dest], sem)
             copy.start()
             copy.wait()
-            return carry
-
-        lax.fori_loop(0, dests, one_dest, 0)
 
     smem = pl.BlockSpec(memory_space=pltpu.SMEM)
     return pl.pallas_call(
@@ -245,12 +272,11 @@
         out_specs=pl.BlockSpec(memory_space=pl.ANY),
         scratch_shapes=[
             pltpu.VMEM(((per_dest + 1) * cols, LANES), jnp.float32),
-            pltpu.SMEM((slots,), jnp.int32),
             pltpu.SemaphoreType.DMA,
         ],
         compiler_params=pltpu.CompilerParams(vmem_limit_bytes=16 << 20),
         name="pack_rest",
-    )(lengths, prompts, u)
+    )(slot_of, lengths, u)
 
 
 def score_kernel(members, per_dest, cols, scales, refs):
@@ -264,21 +290,18 @@
             [main[k * chunk + i : k * chunk + i + 1, :] for k in range(members)], axis=0
         )
 
-    reward = field(1)
+    start = lax.rem(lax.axis_index(GY) * per_dest, LANES)
+    shift = lax.rem(LANES - start, LANES)
+    lengths, reward, sums_p, sums_q = (pltpu.roll(field(i), shift, 1) for i in range(4))
     total = jnp.sum(reward, axis=0, keepdims=True)
     advantage = (members * reward - total) / (members - 1)
     tokens = jnp.sum(field(4), axis=0, keepdims=True)
     scale = grad_scale / tokens
-    table_ref[0] = field(0)
+    table_ref[0] = lengths
     table_ref[1] = -advantage * scale
     table_ref[2] = jnp.broadcast_to(scale * -KL, (members, LANES))
     to_scalars = pltpu.make_async_copy(table_ref, numbers, num_sem)
     to_scalars.start()
-
-    start = lax.rem(lax.axis_index(GY) * per_dest, LANES)
-    shift = lax.rem(LANES - start, LANES)
-    sums_p = pltpu.roll(field(2), shift, 1)
-    sums_q = pltpu.roll(field(3), shift, 1)
     loss = (KL * sums_q - advantage * sums_p) * (loss_scale / tokens)
     loss_ref[...] = loss[:, 0:per_dest]
     adv_ref[...] = advantage[:, 0:per_dest]
@@ -419,7 +442,7 @@
 def peers(x, axis):
     size = lax.axis_size(axis)
     return [
-        lax.ppermute(x, axis, [(i, (i + step) % size) for i in range(size)])
+        lax.ppermute(x, axis, [(i, i ^ step) for i in range(size)])
         for step in range(1, size)
     ]
 
@@ -433,19 +456,21 @@
     samples = members * slots * lax.axis_size(GX)
     scales = (float(samples * seq_slots), float(samples))
     tokens = [lengths] + peers(lengths, GX)
-    u, sums_p, sums_q = token_terms(
-        lengths,
-        pltpu.with_memory_space_constraint(policy_logp[0], pltpu.HBM),
-        pltpu.with_memory_space_constraint(anchor_logp[0], pltpu.HBM),
+    u, sums, slot_of = token_terms(
+        *(
+            pltpu.with_memory_space_constraint(x, pltpu.HBM)
+            for x in (lengths, rewards, slot_prompt, policy_logp[0], anchor_logp[0])
+        ),
+        dests,
     )
     u = lane_rows(u, slots, seq_slots)
-    main = pack(lengths, rewards, slot_prompt, tokens, u, sums_p, sums_q, dests)
+    main = pack(slot_of, lengths, tokens, u, sums, dests)
     main = lax.all_to_all(main, GY, 0, 0, tiled=True)
     grad, loss, advantage, table, more = score(main, scales, per_dest, cols)
 
     def the_rest(state):
         grad, _ = state
-        rest = pack_rest(lengths, slot_prompt, u, dests)
+        rest = pack_rest(slot_of, lengths, u, dests)
         got = lax.all_to_all(rest, GY, 0, 0, tiled=True)
         return finish(grad, got, table, per_dest, cols), jnp.int32(0)
 

time: 75.7 us -> 73.3 us (0.968)
  Pallas kernels: 12.5 us -> 11 us
    pallas_call x1, Pallas kernels: 4.08 us -> 2.74 us  [pack(): pl.pallas_call(body, out_shape=jax.ShapeDtypeStruct((dests * chunk, LANES...]
where the time goes in v3:
time: 73.3 us; the launch traced here: 73.1 us
  blocking collectives  51.3 us (70%)
  Pallas kernels  11 us (15%)
  starting transfers between devices  9.42 us (13%)
    all_to_all x1, blocking collectives, body(): main = lax.all_to_all(main, GY, 0, 0, tiled=True)  51.3 us
    ppermute x7, starting transfers between devices, peers(): lax.ppermute(x, axis, [(i, i ^ step) for i in range(size)])  9.42 us
    pallas_call x1, Pallas kernels, token_terms(): pl.pallas_call(body, out_shape=(jax.ShapeDtypeStruct((slots, width), jnp....  4.39 us
    pallas_call x1, Pallas kernels, score(): pl.pallas_call(body, out_shape=(jax.ShapeDtypeStruct((members * full, LAN...  3.86 us
    pallas_call x1, Pallas kernels, pack(): pl.pallas_call(body, out_shape=jax.ShapeDtypeStruct((dests * chunk, LANES...  2.74 us
  transfers between devices with their start and end apart: 7, of which 0 were waited for; matrix products, arithmetic and copies ran while one was open for 0% of the time, Pallas kernels for 6%

profile of v3, /device:TPU:0, one launch (start us, length us, event | category | flops | bytes accessed | tf_op | source)
XLA Modules:
  0.0 73.1 jit_solution(7657101813887170924)
XLA Ops:
  0.6 0.1 collective-permute-start
  0.7 2.1 %collective-permute-start.1 = (s32[1,256]{1,0:T(1,128)}, s32[1,256]{1,0:T(1,128)S(1)}, u32[]{:S(2)}, u32[]{:S(2)}) collective-permute-start(s32[1,256]{1,0:T(1,128)} %refs_2_.3), channel_id=1, source_target_pairs={{0,32},{16,48},{32,0},{48,16},{64,96},{80,112},{96,64},{112,80},{1... | collective-permute-start | bytes 3080 | tf_op jit(solution)/shard_map/ppermute | solution.py:445
  2.8 0.0 collective-permute-start.2
  2.9 3.7 %collective-permute-start.3 = (s32[1,256]{1,0:T(1,128)}, s32[1,256]{1,0:T(1,128)S(1)}, u32[]{:S(2)}, u32[]{:S(2)}) collective-permute-start(s32[1,256]{1,0:T(1,128)} %refs_2_.3), channel_id=1, source_target_pairs={{0,64},{16,80},{32,96},{48,112},{64,0},{80,16},{96,32},{112,48},{1... | collective-permute-start | bytes 3080 | tf_op jit(solution)/shard_map/ppermute | solution.py:445
  6.6 0.0 collective-permute-start.4
  6.6 0.0 collective-permute-done.refs_3_
  6.6 3.4 %collective-permute-start.5 = (s32[1,256]{1,0:T(1,128)}, s32[1,256]{1,0:T(1,128)S(1)}, u32[]{:S(2)}, u32[]{:S(2)}) collective-permute-start(s32[1,256]{1,0:T(1,128)} %refs_2_.3), channel_id=1, source_target_pairs={{0,96},{16,112},{32,64},{48,80},{64,32},{80,48},{96,0},{112,16},{1... | collective-permute-start | bytes 3080 | tf_op jit(solution)/shard_map/ppermute | solution.py:445
  10.0 0.0 collective-permute-done.1.refs_4_
  10.0 0.1 collective-permute-start.6
  10.1 0.0 copy-start.1
  10.1 4.4 %token_terms.1 = (f32[256,4096]{1,0:T(8,128)S(1)}, f32[256,128]{1,0:T(8,128)S(1)}, s32[1,256]{1,0:T(1,128)S(1)}) custom-call(s32[1,256]{1,0:T(1,128)} %refs_0_.1, s32[1,256]{1,0:T(1,128)} %refs_2_.3, s32[1,256]{1,0:T(1,128)} %refs_2_.2, f32[256,4096]{1,0:T(8,128)} %bitcast.21, f32[256,4096]{1,0:T(8,128)} %bitcast.22), custom_call_target="tpu_custom_call" | custom-call | flops 40000000 | bytes 12582912 | tf_op jit(solution)/shard_map/token_terms/pallas_call | solution.py:135
  14.5 0.0 copy-start
  14.5 0.0 collective-permute-done.2.refs_5_
  14.5 0.0 collective-permute-done.3.refs_6_
  14.5 0.0 collective-permute-done.4.refs_7_
  14.5 0.0 collective-permute-done.5.refs_8_
  14.5 0.0 collective-permute-done.6.refs_9_
  14.5 0.0 copy-done.1
  14.5 2.7 %pack.1 = f32[7040,128]{1,0:T(8,128)S(1)} custom-call(s32[1,256]{1,0:T(1,128)S(1)} %get-tuple-element.71.refs_0_, s32[1,256]{1,0:T(1,128)S(1)} %copy-done.1, s32[1,256]{1,0:T(1,128)S(1)} %copy-done.1, s32[1,256]{1,0:T(1,128)S(1)} %collective-permute-done.refs_3_, s32[1,256]{1,0:T(1,128)S(1)} %collective-permute-done.1.refs_4_, ...), custom_call_target="tpu_custom_call" | custom-call | tf_op jit(solution)/shard_map/pack/pallas_call | solution.py:233
  17.3 0.0 copy-done
  17.3 51.3 %all_to_all.9 = f32[16,440,128]{2,1,0:T(8,128)S(1)} all-to-all(f32[16,440,128]{2,1,0:T(8,128)S(1)} %bitcast.16), channel_id=1, replica_groups=mesh['gx_0'=4,'gx_1'=2,'gy_0'=4,'gy_1'=4] {'gy_0','gy_1'}, dimensions={0} | all-to-all | bytes 7208960 | tf_op jit(solution)/shard_map/all_to_all | solution.py:468
  68.6 3.9 %score.1 = (f32[8192,128]{1,0:T(8,128)}, f32[16,16]{1,0:T(8,128)}, f32[16,16]{1,0:T(8,128)}, f32[3,16,128]{2,1,0:T(8,128)S(1)}, s32[1,128]{1,0:T(1,128)}) custom-call(f32[7040,128]{1,0:T(8,128)S(1)} %bitcast.17), custom_call_target="tpu_custom_call" | custom-call | tf_op jit(solution)/shard_map/score/pallas_call | solution.py:352
  72.5 0.6 while.9
Async XLA Ops:
  0.6 5.9 %collective-permute-start = (s32[1,256]{1,0:T(1,128)}, s32[1,256]{1,0:T(1,128)S(1)}, u32[]{:S(2)}, u32[]{:S(2)}) collective-permute-start(s32[1,256]{1,0:T(1,128)} %refs_2_.3), channel_id=1, source_target_pairs={{0,16},{16,0},{32,48},{48,32},{64,80},{80,64},{96,112},{112,96},{1... | collective-permute-start | bytes 3080 | tf_op jit(solution)/shard_map/ppermute | solution.py:445
  0.7 9.2 %collective-permute-start.1 = (s32[1,256]{1,0:T(1,128)}, s32[1,256]{1,0:T(1,128)S(1)}, u32[]{:S(2)}, u32[]{:S(2)}) collective-permute-start(s32[1,256]{1,0:T(1,128)} %refs_2_.3), channel_id=1, source_target_pairs={{0,32},{16,48},{32,0},{48,16},{64,96},{80,112},{96,64},{112,80},{1... | collective-permute-start | bytes 3080 | tf_op jit(solution)/shard_map/ppermute | solution.py:445
  2.8 11.6 %collective-permute-start.2 = (s32[1,256]{1,0:T(1,128)}, s32[1,256]{1,0:T(1,128)S(1)}, u32[]{:S(2)}, u32[]{:S(2)}) collective-permute-start(s32[1,256]{1,0:T(1,128)} %refs_2_.3), channel_id=1, source_target_pairs={{0,48},{16,32},{32,16},{48,0},{64,112},{80,96},{96,80},{112,64},{1... | collective-permute-start | bytes 3080 | tf_op jit(solution)/shard_map/ppermute | solution.py:445
  2.9 11.6 %collective-permute-start.3 = (s32[1,256]{1,0:T(1,128)}, s32[1,256]{1,0:T(1,128)S(1)}, u32[]{:S(2)}, u32[]{:S(2)}) collective-permute-start(s32[1,256]{1,0:T(1,128)} %refs_2_.3), channel_id=1, source_target_pairs={{0,64},{16,80},{32,96},{48,112},{64,0},{80,16},{96,32},{112,48},{1... | collective-permute-start | bytes 3080 | tf_op jit(solution)/shard_map/ppermute | solution.py:445
  6.6 7.9 %collective-permute-start.4 = (s32[1,256]{1,0:T(1,128)}, s32[1,256]{1,0:T(1,128)S(1)}, u32[]{:S(2)}, u32[]{:S(2)}) collective-permute-start(s32[1,256]{1,0:T(1,128)} %refs_2_.3), channel_id=1, source_target_pairs={{0,80},{16,64},{32,112},{48,96},{64,16},{80,0},{96,48},{112,32},{1... | collective-permute-start | bytes 3080 | tf_op jit(solution)/shard_map/ppermute | solution.py:445
  6.6 7.9 %collective-permute-start.5 = (s32[1,256]{1,0:T(1,128)}, s32[1,256]{1,0:T(1,128)S(1)}, u32[]{:S(2)}, u32[]{:S(2)}) collective-permute-start(s32[1,256]{1,0:T(1,128)} %refs_2_.3), channel_id=1, source_target_pairs={{0,96},{16,112},{32,64},{48,80},{64,32},{80,48},{96,0},{112,16},{1... | collective-permute-start | bytes 3080 | tf_op jit(solution)/shard_map/ppermute | solution.py:445
  10.0 4.6 %collective-permute-start.6 = (s32[1,256]{1,0:T(1,128)}, s32[1,256]{1,0:T(1,128)S(1)}, u32[]{:S(2)}, u32[]{:S(2)}) collective-permute-start(s32[1,256]{1,0:T(1,128)} %refs_2_.3), channel_id=1, source_target_pairs={{0,112},{16,96},{32,80},{48,64},{64,48},{80,32},{96,16},{112,0},{1... | collective-permute-start | bytes 3080 | tf_op jit(solution)/shard_map/ppermute | solution.py:445
  10.1 4.5 %copy-start.1 = (s32[1,256]{1,0:T(1,128)S(1)}, s32[1,256]{1,0:T(1,128)}, u32[]{:S(2)}) copy-start(s32[1,256]{1,0:T(1,128)} %refs_2_.3) | copy-start | bytes 3076
  14.5 2.8 %copy-start = (f32[256,4096]{1,0:T(8,128)}, f32[256,4096]{1,0:T(8,128)S(1)}, u32[]{:S(2)}) copy-start(f32[256,4096]{1,0:T(8,128)S(1)} %get-tuple-element.43) | copy-start | bytes 12582916

commit v4 on v3

--- a/solution.py
+++ b/solution.py
@@ -14,14 +14,6 @@
 LANES = 128
 META = 8
 FAST = 432
-
-
-def lane_rows(x, rows, width):
-    return (
-        x.reshape(rows // 8, 8, width // LANES, LANES)
-        .transpose(0, 2, 1, 3)
-        .reshape(rows * width // LANES, LANES)
-    )
 
 
 def sliced_position(cols):
@@ -67,9 +59,9 @@
         pltpu.make_async_copy(src, dst, small_sem.at[i])
         for i, (src, dst) in enumerate(zip(small_hbm, (prompt_ref, len_ref, reward_ref)))
     ]
-    for load in (*loads(0), *small):
+    for load in small:
         load.start()
-    for step in range(1, STEPS):
+    for step in range(STEPS):
         for load in loads(step):
             load.start()
     for load in small:
@@ -108,7 +100,7 @@
                 d = anchor[at] - a
                 valid = behind < -c * LANES
                 u = jnp.where(valid, jnp.exp(d) - 1.0, 0.0)
-                u_ref[at] = u
+                u_ref[pl.ds(first * cols + c // 8 * 64 + c % 8, 8, stride=8), :] = u
                 sums_q[c % 4] = sums_q[c % 4] + (u - jnp.where(valid, d, 0.0))
                 sums_p[c % 4] = sums_p[c % 4] + jnp.where(valid, a, 0.0)
             parts[0, pl.ds(first, 8), :] = (sums_p[0] + sums_p[1]) + (sums_p[2] + sums_p[3])
@@ -135,7 +127,7 @@
     return pl.pallas_call(
         body,
         out_shape=(
-            jax.ShapeDtypeStruct((slots, width), jnp.float32),
+            jax.ShapeDtypeStruct((slots * width // LANES, LANES), jnp.float32),
             jax.ShapeDtypeStruct((slots, LANES), jnp.float32),
             jax.ShapeDtypeStruct((1, slots), jnp.int32),
         ),
@@ -165,10 +157,10 @@
     cols,
     slot_of,
     len_ref,
-    tok_refs,
     u_ref,
     sums_ref,
     main,
+    head_ref,
     stage,
     in_order,
 ):
@@ -180,8 +172,9 @@
         def row(r, at):
             p = dest * per_dest + r
             s = slot_of[0, p]
-            first = (s >> 3) * (8 * cols) + (s & 7)
-            ref[pl.ds(at, cols), :] = u_ref[pl.ds(first, cols, stride=8), :]
+            first = pl.multiple_of((s >> 3) * (8 * cols) + (s & 7) * 8, 8)
+            for j in range(cols // 8):
+                ref[pl.ds(at + 8 * j, 8), :] = u_ref[pl.ds(first + 64 * j, 8), :]
             in_order[pl.ds(p, 1), :] = sums_ref[pl.ds(s, 1), :]
             return at + ((len_ref[0, s] + (LANES - 1)) >> 7)
 
@@ -208,16 +201,67 @@
         precision=lax.Precision.HIGHEST,
         preferred_element_type=jnp.float32,
     )
-    tokens = jnp.sum(sum(t[...] for t in tok_refs).astype(jnp.float32), axis=1, keepdims=True)
     sub = lax.broadcasted_iota(jnp.int32, (8, slots), 0)
-    head = jnp.where(sub == 4, tokens, head)
-    head = jnp.where(sub == 5, most.astype(jnp.float32), head)
-    for dest in range(dests):
-        half = dest * per_dest // LANES * LANES
-        main[dest * chunk : dest * chunk + META, :] = head[:, half : half + LANES]
-
-
-def pack(slot_of, lengths, tokens, u, sums, dests):
+    head_ref[...] = jnp.where(sub == 5, most.astype(jnp.float32), head)
+
+
+def stamp_kernel(dests, per_dest, head, counts, _, main, tile, sem):
+    sub = lax.broadcasted_iota(jnp.int32, (8, LANES), 0)
+    count = jnp.sum(sum(c[...] for c in counts).astype(jnp.float32), axis=1, keepdims=True)
+    halves = head.shape[1] // LANES
+    for half in range(halves):
+        tile[half] = jnp.where(sub == 4, count, head[:, half * LANES : (half + 1) * LANES])
+    copies = [
+        pltpu.make_async_copy(
+            tile.at[dest * per_dest // LANES], main.at[dest, pl.ds(0, META)], sem.at[dest]
+        )
+        for dest in range(dests)
+    ]
+    for copy in copies:
+        copy.start()
+    for copy in copies:
+        copy.wait()
+
+
+def stamp(head, counts, main, per_dest):
+    dests = main.shape[0]
+    vmem = pl.BlockSpec(memory_space=pltpu.VMEM)
+    place = pl.BlockSpec(memory_space=pl.ANY)
+
+    def body(head, *refs):
+        stamp_kernel(dests, per_dest, head, refs[: len(counts)], *refs[len(counts) :])
+
+    return pl.pallas_call(
+        body,
+        out_shape=jax.ShapeDtypeStruct(main.shape, jnp.float32),
+        in_specs=[vmem] * (1 + len(counts)) + [place],
+        out_specs=place,
+        input_output_aliases={1 + len(counts): 0},
+        scratch_shapes=[
+            pltpu.VMEM((head.shape[1] // LANES, META, LANES), jnp.float32),
+            pltpu.SemaphoreType.DMA((dests,)),
+        ],
+        compiler_params=pltpu.CompilerParams(vmem_limit_bytes=4 << 20),
+        name="stamp",
+    )(head, *counts, main)
+
+
+def added(x, y, after):
+    def body(x, y, _, out):
+        out[...] = x[...] + y[...]
+
+    vmem = pl.BlockSpec(memory_space=pltpu.VMEM)
+    return pl.pallas_call(
+        body,
+        out_shape=jax.ShapeDtypeStruct(x.shape, x.dtype),
+        in_specs=[vmem, vmem, pl.BlockSpec(memory_space=pl.ANY)],
+        out_specs=vmem,
+        compiler_params=pltpu.CompilerParams(vmem_limit_bytes=4 << 20),
+        name="added",
+    )(x, y, after)
+
+
+def pack(slot_of, lengths, u, sums, dests):
     slots = lengths.shape[1]
     per_dest = slots // dests
     cols = u.shape[0] // slots
@@ -226,22 +270,27 @@
     vmem = pl.BlockSpec(memory_space=pltpu.VMEM)
 
     def body(*refs):
-        small, refs = refs[:2], refs[2:]
-        tok_refs, refs = refs[: len(tokens)], refs[len(tokens) :]
-        pack_kernel(dests, per_dest, cols, *small, tok_refs, *refs)
-
-    return pl.pallas_call(
-        body,
-        out_shape=jax.ShapeDtypeStruct((dests * chunk, LANES), jnp.float32),
-        in_specs=[smem] * 2 + [vmem] * (len(tokens) + 2),
-        out_specs=vmem,
+        pack_kernel(dests, per_dest, cols, *refs)
+
+    main, head = pl.pallas_call(
+        body,
+        out_shape=(
+            jax.ShapeDtypeStruct((dests * chunk, LANES), jnp.float32),
+            jax.ShapeDtypeStruct((META, slots), jnp.float32),
+        ),
+        in_specs=[smem] * 2 + [vmem] * 2,
+        out_specs=(vmem, vmem),
         scratch_shapes=[
             pltpu.VMEM((META + (per_dest + 1) * cols, LANES), jnp.float32),
             pltpu.VMEM((slots, LANES), jnp.float32),
         ],
         compiler_params=pltpu.CompilerParams(vmem_limit_bytes=24 << 20),
+        cost_estimate=pl.CostEstimate(
+            flops=40_000_000, bytes_accessed=8 * dests * chunk * LANES, transcendentals=0
+        ),
         name="pack",
-    )(slot_of, lengths, *tokens, u, sums).reshape(dests, chunk, LANES)
+    )(slot_of, lengths, u, sums)
+    return main.reshape(dests, chunk, LANES), head
 
 
 def pack_rest(slot_of, lengths, u, dests):
@@ -255,8 +304,9 @@
         def _(dest):
             def row(r, at):
                 s = slot_of[0, dest * per_dest + r]
-                first = (s >> 3) * (8 * cols) + (s & 7)
-                stage[pl.ds(at, cols), :] = u_ref[pl.ds(first, cols, stride=8), :]
+                first = pl.multiple_of((s >> 3) * (8 * cols) + (s & 7) * 8, 8)
+                for j in range(cols // 8):
+                    stage[pl.ds(at + 8 * j, 8), :] = u_ref[pl.ds(first + 64 * j, 8), :]
                 return at + ((len_ref[0, s] + (LANES - 1)) >> 7)
 
             lax.fori_loop(0, per_dest, row, jnp.int32(0))
@@ -455,7 +505,7 @@
     members = members_dev * dests
     samples = members * slots * lax.axis_size(GX)
     scales = (float(samples * seq_slots), float(samples))
-    tokens = [lengths] + peers(lengths, GX)
+    other = peers(lengths, "gx_1")[0]
     u, sums, slot_of = token_terms(
         *(
             pltpu.with_memory_space_constraint(x, pltpu.HBM)
@@ -463,8 +513,9 @@
         ),
         dests,
     )
-    u = lane_rows(u, slots, seq_slots)
-    main = pack(slot_of, lengths, tokens, u, sums, dests)
+    pair = added(lengths, other, slot_of)
+    main, head = pack(slot_of, lengths, u, sums, dests)
+    main = stamp(head, [pair] + peers(pair, "gx_0"), main, per_dest)
     main = lax.all_to_all(main, GY, 0, 0, tiled=True)
     grad, loss, advantage, table, more = score(main, scales, per_dest, cols)
 

time: 73.3 us -> 71 us (0.969)
  starting transfers between devices: 9.42 us -> 5.78 us
  waiting for transfers between devices: 0.02 us -> 2.59 us
  blocking collectives: 51.3 us -> 50.3 us
    ppermute x7 -> x4, starting transfers between devices: 9.42 us -> 5.78 us  [peers(): lax.ppermute(x, axis, [(i, i ^ step) for i in range(size)])]
    ppermute x7 -> x4, waiting for transfers between devices: 0.02 us -> 2.59 us  [peers(): lax.ppermute(x, axis, [(i, i ^ step) for i in range(size)])]
    all_to_all x1, blocking collectives: 51.3 us -> 50.3 us  [body(): main = lax.all_to_all(main, GY, 0, 0, tiled=True)]
    pallas_call x2 -> x4, Pallas kernels: 7.13 us -> 6.92 us  [the longest x1 4.4 us: token_terms(): pl.pallas_call(body, out_shape=(jax.ShapeDtypeStruct((slots * width // LA...]
  transfers between devices with their start and end apart: 7 -> 4, of which waited for: 0 -> 1; matrix products, arithmetic and copies ran while one was open for 0% -> 0% of each run, Pallas kernels for 6% -> 9%
where the time goes in v4:
time: 71 us; the launch traced here: 70.8 us
  blocking collectives  50.3 us (71%)
  Pallas kernels  10.8 us (15%)
  starting transfers between devices  5.78 us (8%)
  waiting for transfers between devices  2.59 us (4%)
  between operations  0.71 us (1%)
    all_to_all x1, blocking collectives, body(): main = lax.all_to_all(main, GY, 0, 0, tiled=True)  50.3 us
    ppermute x4, starting transfers between devices, peers(): lax.ppermute(x, axis, [(i, i ^ step) for i in range(size)])  5.78 us
    pallas_call x1, Pallas kernels, token_terms(): pl.pallas_call(body, out_shape=(jax.ShapeDtypeStruct((slots * width // LA...  4.4 us
    pallas_call x1, Pallas kernels, score(): pl.pallas_call(body, out_shape=(jax.ShapeDtypeStruct((members * full, LAN...  3.86 us
    ppermute x4, waiting for transfers between devices, peers(): lax.ppermute(x, axis, [(i, i ^ step) for i in range(size)])  2.59 us
    pallas_call x1, Pallas kernels, pack(): pl.pallas_call(body, out_shape=(jax.ShapeDtypeStruct((dests * chunk, LANE...  2.19 us
  transfers between devices with their start and end apart: 4, of which 1 were waited for; matrix products, arithmetic and copies ran while one was open for 0% of the time, Pallas kernels for 9%

profile of v4, /device:TPU:0, one launch (start us, length us, event | category | flops | bytes accessed | tf_op | source)
XLA Modules:
  0.0 70.8 jit_solution(13350609086243736538)
XLA Ops:
  0.6 0.1 collective-permute-start
  0.7 0.0 copy-start.1
  0.7 4.4 %token_terms.1 = (f32[8192,128]{1,0:T(8,128)S(1)}, f32[256,128]{1,0:T(8,128)S(1)}, s32[1,256]{1,0:T(1,128)S(1)}) custom-call(s32[1,256]{1,0:T(1,128)} %refs_0_.1, s32[1,256]{1,0:T(1,128)} %x.1, s32[1,256]{1,0:T(1,128)} %refs_2_.1, f32[256,4096]{1,0:T(8,128)} %bitcast.14, f32[256,4096]{1,0:T(8,128)} %bitcast.15), custom_call_target="tpu_custom_call" | custom-call | flops 40000000 | bytes 12582912 | tf_op jit(solution)/shard_map/token_terms/pallas_call | solution.py:127
  5.1 0.0 copy-start
  5.2 0.0 collective-permute-done.y
  5.2 0.0 copy-done.1
  5.2 2.1 %collective-permute-start.1 = (s32[1,256]{1,0:T(1,128)S(1)}, s32[1,256]{1,0:T(1,128)S(1)}, u32[]{:S(2)}, u32[]{:S(2)}) collective-permute-start(s32[1,256]{1,0:T(1,128)S(1)} %added.1.refs_0_), channel_id=1, source_target_pairs={{0,32},{32,0},{64,96},{96,64},{1,33},{33,1},{65,97},{97,65},{2,34}... | collective-permute-start | bytes 3080 | tf_op jit(solution)/shard_map/ppermute | solution.py:495
  7.3 3.6 %collective-permute-start.2 = (s32[1,256]{1,0:T(1,128)S(1)}, s32[1,256]{1,0:T(1,128)S(1)}, u32[]{:S(2)}, u32[]{:S(2)}) collective-permute-start(s32[1,256]{1,0:T(1,128)S(1)} %added.1.refs_0_), channel_id=1, source_target_pairs={{0,64},{32,96},{64,0},{96,32},{1,65},{33,97},{65,1},{97,33},{2,66}... | collective-permute-start | bytes 3080 | tf_op jit(solution)/shard_map/ppermute | solution.py:495
  10.9 0.0 collective-permute-start.3
  10.9 2.2 %pack.1 = (f32[7040,128]{1,0:T(8,128)S(1)}, f32[8,256]{1,0:T(8,128)S(1)}) custom-call(s32[1,256]{1,0:T(1,128)S(1)} %get-tuple-element.75.refs_0_._, s32[1,256]{1,0:T(1,128)S(1)} %copy-done.1, f32[8192,128]{1,0:T(8,128)S(1)} %get-tuple-element.77.refs_2_, f32[256,128]{1,0:T(8,128)S(1)} %get-tuple-element.46.refs_3_), custom_call_target="tpu_custom_call" | custom-call | flops 40000000 | bytes 7208960 | tf_op jit(solution)/shard_map/pack/pallas_call | solution.py:275
  13.1 0.0 collective-permute-done.1.refs_1_
  13.1 0.0 collective-permute-done.2.refs_2_
  13.1 2.6 %collective-permute-done.3.refs_3_ = s32[1,256]{1,0:T(1,128)S(1)} collective-permute-done((s32[1,256]{1,0:T(1,128)S(1)}, s32[1,256]{1,0:T(1,128)S(1)}, u32[]{:S(2)}, u32[]{:S(2)}) %collective-permute-start.3) | collective-permute-done | bytes 1056 | tf_op jit(solution)/shard_map/ppermute | solution.py:495
  15.7 0.0 copy-done
  15.7 0.3 stamp.1
  16.0 50.3 %all_to_all.9 = f32[16,440,128]{2,1,0:T(8,128)S(1)} all-to-all(f32[16,440,128]{2,1,0:T(8,128)S(1)} %stamp.1), channel_id=1, replica_groups=mesh['gx_0'=4,'gx_1'=2,'gy_0'=4,'gy_1'=4] {'gy_0','gy_1'}, dimensions={0} | all-to-all | bytes 7208960 | tf_op jit(solution)/shard_map/all_to_all | solution.py:519
  66.3 3.9 %score.1 = (f32[8192,128]{1,0:T(8,128)}, f32[16,16]{1,0:T(8,128)}, f32[16,16]{1,0:T(8,128)}, f32[3,16,128]{2,1,0:T(8,128)S(1)}, s32[1,128]{1,0:T(1,128)}) custom-call(f32[7040,128]{1,0:T(8,128)S(1)} %bitcast.11), custom_call_target="tpu_custom_call" | custom-call | tf_op jit(solution)/shard_map/score/pallas_call | solution.py:402
  70.1 0.7 while.9
  (1 shorter events, 0.0 us)
Async XLA Ops:
  0.6 4.5 %collective-permute-start = (s32[1,256]{1,0:T(1,128)}, s32[1,256]{1,0:T(1,128)S(1)}, u32[]{:S(2)}, u32[]{:S(2)}) collective-permute-start(s32[1,256]{1,0:T(1,128)} %x.1), channel_id=1, source_target_pairs={{0,16},{16,0},{1,17},{17,1},{2,18},{18,2},{3,19},{19,3},{4,20},{20... | collective-permute-start | bytes 3080 | tf_op jit(solution)/shard_map/ppermute | solution.py:495
  0.7 4.4 %copy-start.1 = (s32[1,256]{1,0:T(1,128)S(1)}, s32[1,256]{1,0:T(1,128)}, u32[]{:S(2)}) copy-start(s32[1,256]{1,0:T(1,128)} %x.1) | copy-start | bytes 3076
  5.1 10.5 %copy-start = (f32[8192,128]{1,0:T(8,128)}, f32[8192,128]{1,0:T(8,128)S(1)}, u32[]{:S(2)}) copy-start(f32[8192,128]{1,0:T(8,128)S(1)} %get-tuple-element.77.refs_2_) | copy-start | bytes 12582916
  5.2 7.9 %collective-permute-start.1 = (s32[1,256]{1,0:T(1,128)S(1)}, s32[1,256]{1,0:T(1,128)S(1)}, u32[]{:S(2)}, u32[]{:S(2)}) collective-permute-start(s32[1,256]{1,0:T(1,128)S(1)} %added.1.refs_0_), channel_id=1, source_target_pairs={{0,32},{32,0},{64,96},{96,64},{1,33},{33,1},{65,97},{97,65},{2,34}... | collective-permute-start | bytes 3080 | tf_op jit(solution)/shard_map/ppermute | solution.py:495
  7.3 5.8 %collective-permute-start.2 = (s32[1,256]{1,0:T(1,128)S(1)}, s32[1,256]{1,0:T(1,128)S(1)}, u32[]{:S(2)}, u32[]{:S(2)}) collective-permute-start(s32[1,256]{1,0:T(1,128)S(1)} %added.1.refs_0_), channel_id=1, source_target_pairs={{0,64},{32,96},{64,0},{96,32},{1,65},{33,97},{65,1},{97,33},{2,66}... | collective-permute-start | bytes 3080 | tf_op jit(solution)/shard_map/ppermute | solution.py:495
  10.9 4.8 %collective-permute-start.3 = (s32[1,256]{1,0:T(1,128)S(1)}, s32[1,256]{1,0:T(1,128)S(1)}, u32[]{:S(2)}, u32[]{:S(2)}) collective-permute-start(s32[1,256]{1,0:T(1,128)S(1)} %added.1.refs_0_), channel_id=1, source_target_pairs={{0,96},{32,64},{64,32},{96,0},{1,97},{33,65},{65,33},{97,1},{2,98}... | collective-permute-start | bytes 3080 | tf_op jit(solution)/shard_map/ppermute | solution.py:495

commit v5 on v4

--- a/solution.py
+++ b/solution.py
@@ -22,7 +22,7 @@
 
 
 SPAN = LANES // 4
-LEN, REWARD = 2 * SPAN, 3 * SPAN
+LEN, SUM_P, REWARD, SUM_Q = (i * SPAN for i in range(4))
 STEPS = 8
 
 
@@ -33,13 +33,14 @@
     anchor_hbm,
     u_ref,
     sums_ref,
-    slot_of,
+    slot_hbm,
     policy,
     anchor,
     parts,
     len_ref,
     reward_ref,
     prompt_ref,
+    slot_of,
     sem,
     small_sem,
 ):
@@ -72,6 +73,8 @@
         return carry
 
     lax.fori_loop(0, slots, invert, 0, unroll=16)
+    inverse = pltpu.make_async_copy(slot_of, slot_hbm, small_sem.at[3])
+    inverse.start()
     lane = lax.broadcasted_iota(jnp.int32, (8, LANES), 1)
     sub = lax.broadcasted_iota(jnp.int32, (8, LANES), 0)
 
@@ -88,7 +91,7 @@
             for i in range(1, 8):
                 length = jnp.where(sub == i, len_ref[0, first + i], length)
                 reward = jnp.where(sub == i, reward_ref[0, first + i], reward)
-            sums_ref[pl.ds(first, 8), :] = jnp.where(lane < LEN + SPAN, length, reward).astype(
+            sums_ref[pl.ds(first, 8), :] = jnp.where(lane < REWARD, length, reward).astype(
                 jnp.float32
             )
             behind = lane - length
@@ -99,26 +102,25 @@
                 a = policy[at]
                 d = anchor[at] - a
                 valid = behind < -c * LANES
-                u = jnp.where(valid, jnp.exp(d) - 1.0, 0.0)
+                u = jnp.exp(d) - 1.0
                 u_ref[pl.ds(first * cols + c // 8 * 64 + c % 8, 8, stride=8), :] = u
-                sums_q[c % 4] = sums_q[c % 4] + (u - jnp.where(valid, d, 0.0))
+                sums_q[c % 4] = sums_q[c % 4] + jnp.where(valid, u - d, 0.0)
                 sums_p[c % 4] = sums_p[c % 4] + jnp.where(valid, a, 0.0)
             parts[0, pl.ds(first, 8), :] = (sums_p[0] + sums_p[1]) + (sums_p[2] + sums_p[3])
             parts[1, pl.ds(first, 8), :] = (sums_q[0] + sums_q[1]) + (sums_q[2] + sums_q[3])
 
+    inverse.wait()
     lane = lax.broadcasted_iota(jnp.int32, (slots, LANES), 1)
-    p, q = (
-        x + pltpu.roll(x, SPAN, 1)
-        for x in (x + pltpu.roll(x, 2 * SPAN, 1) for x in (parts[0], parts[1]))
-    )
-    rest = jnp.where(lane < 2 * SPAN, q, sums_ref[...])
-    sums_ref[...] = jnp.where(lane < SPAN, p, rest)
+    p, q = (x + pltpu.roll(x, 2 * SPAN, 1) for x in (parts[0], parts[1]))
+    both = jnp.where(lane < REWARD, p, q)
+    both = both + pltpu.roll(both, SPAN, 1)
+    summed = (lane >= SUM_P) & (lane < REWARD) | (lane >= SUM_Q)
+    sums_ref[...] = jnp.where(summed, both, sums_ref[...])
 
 
 def token_terms(lengths, rewards, prompts, policy, anchor, dests):
     slots, width = policy.shape
     vmem = pl.BlockSpec(memory_space=pltpu.VMEM)
-    smem = pl.BlockSpec(memory_space=pltpu.SMEM)
     hbm = pl.BlockSpec(memory_space=pl.ANY)
 
     def body(*refs):
@@ -132,7 +134,7 @@
             jax.ShapeDtypeStruct((1, slots), jnp.int32),
         ),
         in_specs=[hbm] * 5,
-        out_specs=(vmem, vmem, smem),
+        out_specs=(vmem, vmem, hbm),
         scratch_shapes=[
             pltpu.VMEM((slots, width), jnp.float32),
             pltpu.VMEM((slots, width), jnp.float32),
@@ -140,8 +142,9 @@
             pltpu.SMEM((1, slots), jnp.int32),
             pltpu.SMEM((1, slots), jnp.int32),
             pltpu.SMEM((1, slots), jnp.int32),
+            pltpu.SMEM((1, slots), jnp.int32),
             pltpu.SemaphoreType.DMA((2, STEPS)),
-            pltpu.SemaphoreType.DMA((3,)),
+            pltpu.SemaphoreType.DMA((4,)),
         ],
         compiler_params=pltpu.CompilerParams(vmem_limit_bytes=24 << 20),
         cost_estimate=pl.CostEstimate(
@@ -192,8 +195,8 @@
     lane = lax.broadcasted_iota(jnp.int32, (8, LANES), 1)
     pick = jnp.where((sub == 0) & (lane == LEN), 1.0, 0.0)
     pick = jnp.where((sub == 1) & (lane == REWARD), 0.25, pick)
-    pick = jnp.where((sub == 2) & (lane < SPAN), 1.0, pick)
-    pick = jnp.where((sub == 3) & (lane >= SPAN) & (lane < 2 * SPAN), 1.0, pick)
+    pick = jnp.where((sub == 2) & (lane >= SUM_P) & (lane < REWARD), 1.0, pick)
+    pick = jnp.where((sub == 3) & (lane >= SUM_Q), 1.0, pick)
     head = lax.dot_general(
         pick,
         in_order[...],
@@ -246,19 +249,19 @@
     )(head, *counts, main)
 
 
-def added(x, y, after):
-    def body(x, y, _, out):
-        out[...] = x[...] + y[...]
+def added(parts, after):
+    def body(*refs):
+        refs[-1][...] = sum(x[...] for x in refs[:-2])
 
     vmem = pl.BlockSpec(memory_space=pltpu.VMEM)
     return pl.pallas_call(
         body,
-        out_shape=jax.ShapeDtypeStruct(x.shape, x.dtype),
-        in_specs=[vmem, vmem, pl.BlockSpec(memory_space=pl.ANY)],
+        out_shape=jax.ShapeDtypeStruct(parts[0].shape, parts[0].dtype),
+        in_specs=[vmem] * len(parts) + [pl.BlockSpec(memory_space=pl.ANY)],
         out_specs=vmem,
         compiler_params=pltpu.CompilerParams(vmem_limit_bytes=4 << 20),
         name="added",
-    )(x, y, after)
+    )(*parts, after)
 
 
 def pack(slot_of, lengths, u, sums, dests):
@@ -330,7 +333,23 @@
 
 
 def score_kernel(members, per_dest, cols, scales, refs):
-    main, grad_hbm, loss_ref, adv_ref, table_ref, more_ref, tail, grad, numbers, num_sem, out_sem = refs
+    (
+        main,
+        grad_hbm,
+        loss_hbm,
+        adv_hbm,
+        table_ref,
+        more_hbm,
+        tail,
+        grad,
+        numbers,
+        loss_ref,
+        adv_ref,
+        more_ref,
+        num_sem,
+        out_sem,
+        small_sem,
+    ) = refs
     grad_scale, loss_scale = scales
     width = per_dest * cols
     chunk = META + FAST
@@ -357,6 +376,14 @@
     adv_ref[...] = advantage[:, 0:per_dest]
     most = jnp.max(field(5), axis=0, keepdims=True)
     more_ref[...] = jnp.where(most > FAST, 1, 0)
+    small = [
+        pltpu.make_async_copy(src, dst, small_sem.at[i])
+        for i, (src, dst) in enumerate(
+            ((loss_ref, loss_hbm), (adv_ref, adv_hbm), (more_ref, more_hbm))
+        )
+    ]
+    for copy in small:
+        copy.start()
     position = sliced_position(cols)
     last = members - 1
     tail[0:chunk, :] = main[last * chunk : (last + 1) * chunk, :]
@@ -384,6 +411,9 @@
 
     one_member(last, tail, 0)
 
+    for copy in small:
+        copy.wait()
+
     @pl.loop(0, members)
     def _(k):
         out_copy(k).wait()
@@ -409,13 +439,17 @@
             jax.ShapeDtypeStruct((1, LANES), jnp.int32),
         ),
         in_specs=[vmem],
-        out_specs=(hbm, vmem, vmem, vmem, vmem),
+        out_specs=(hbm, hbm, hbm, vmem, hbm),
         scratch_shapes=[
             pltpu.VMEM((chunk + cols, LANES), jnp.float32),
             pltpu.VMEM((members * full, LANES), jnp.float32),
             pltpu.SMEM((3, members, LANES), jnp.float32),
+            pltpu.VMEM((members, per_dest), jnp.float32),
+            pltpu.VMEM((members, per_dest), jnp.float32),
+            pltpu.VMEM((1, LANES), jnp.int32),
             pltpu.SemaphoreType.DMA,
             pltpu.SemaphoreType.DMA((members,)),
+            pltpu.SemaphoreType.DMA((3,)),
         ],
         compiler_params=pltpu.CompilerParams(vmem_limit_bytes=24 << 20),
         name="score",
@@ -489,12 +523,9 @@
     )(table, rest, grad)
 
 
-def peers(x, axis):
-    size = lax.axis_size(axis)
-    return [
-        lax.ppermute(x, axis, [(i, i ^ step) for i in range(size)])
-        for step in range(1, size)
-    ]
+def partner(x, step):
+    size = lax.axis_size(GX)
+    return lax.ppermute(x, GX, [(i, i ^ step) for i in range(size)])
 
 
 def body(policy_logp, anchor_logp, lengths, rewards, slot_prompt):
@@ -505,7 +536,7 @@
     members = members_dev * dests
     samples = members * slots * lax.axis_size(GX)
     scales = (float(samples * seq_slots), float(samples))
-    other = peers(lengths, "gx_1")[0]
+    near = [lengths] + [partner(lengths, step) for step in (4, 1, 5)]
     u, sums, slot_of = token_terms(
         *(
             pltpu.with_memory_space_constraint(x, pltpu.HBM)
@@ -513,9 +544,9 @@
         ),
         dests,
     )
-    pair = added(lengths, other, slot_of)
+    near = added(near, slot_of)
     main, head = pack(slot_of, lengths, u, sums, dests)
-    main = stamp(head, [pair] + peers(pair, "gx_0"), main, per_dest)
+    main = stamp(head, [near, partner(near, 2)], main, per_dest)
     main = lax.all_to_all(main, GY, 0, 0, tiled=True)
     grad, loss, advantage, table, more = score(main, scales, per_dest, cols)
 

time: 71 us -> 68.9 us (0.970)
  waiting for transfers between devices: 2.59 us -> 0.82 us
  Pallas kernels: 10.8 us -> 9.8 us
  blocking collectives: 50.3 us -> 51.3 us
    ppermute x4, waiting for transfers between devices: 2.59 us -> 0.82 us  [partner(): return lax.ppermute(x, GX, [(i, i ^ step) for i in range(size)])]
    all_to_all x1, blocking collectives: 50.3 us -> 51.3 us  [body(): main = lax.all_to_all(main, GY, 0, 0, tiled=True)]
  transfers between devices with their start and end apart: 4 -> 4, of which waited for: 1 -> 2; matrix products, arithmetic and copies ran while one was open for 0% -> 0% of each run, Pallas kernels for 9% -> 9%
where the time goes in v5:
time: 68.9 us; the launch traced here: 68.7 us
  blocking collectives  51.3 us (74%)
  Pallas kernels  9.8 us (14%)
  starting transfers between devices  5.39 us (8%)
  waiting for transfers between devices  0.82 us (1%)
  loops' own time  0.69 us (1%)
  between operations  0.69 us (1%)
    all_to_all x1, blocking collectives, body(): main = lax.all_to_all(main, GY, 0, 0, tiled=True)  51.3 us
    ppermute x4, starting transfers between devices, partner(): return lax.ppermute(x, GX, [(i, i ^ step) for i in range(size)])  5.39 us
    pallas_call x1, Pallas kernels, token_terms(): pl.pallas_call(body, out_shape=(jax.ShapeDtypeStruct((slots * width // LA...  4 us
    pallas_call x1, Pallas kernels, score(): pl.pallas_call(body, out_shape=(jax.ShapeDtypeStruct((members * full, LAN...  3.28 us
    pallas_call x1, Pallas kernels, pack(): pl.pallas_call(body, out_shape=(jax.ShapeDtypeStruct((dests * chunk, LANE...  2.19 us
  transfers between devices with their start and end apart: 4, of which 2 were waited for; matrix products, arithmetic and copies ran while one was open for 0% of the time, Pallas kernels for 9%

profile of v5, /device:TPU:0, one launch (start us, length us, event | category | flops | bytes accessed | tf_op | source)
XLA Modules:
  0.0 68.7 jit_solution(5477164007369083999)
XLA Ops:
  0.6 4.1 %collective-permute-start = (s32[1,256]{1,0:T(1,128)}, s32[1,256]{1,0:T(1,128)S(1)}, u32[]{:S(2)}, u32[]{:S(2)}) collective-permute-start(s32[1,256]{1,0:T(1,128)} %refs_0_.3), channel_id=1, source_target_pairs={{0,64},{16,80},{32,96},{48,112},{64,0},{80,16},{96,32},{112,48},{1... | collective-permute-start | bytes 3080 | tf_op jit(solution)/shard_map/ppermute | solution.py:528
  4.7 0.0 collective-permute-start.1
  4.7 0.2 collective-permute-start.2
  4.9 0.0 copy-start.1
  4.9 4.0 %token_terms.1 = (f32[8192,128]{1,0:T(8,128)S(1)}, f32[256,128]{1,0:T(8,128)S(1)}, s32[1,256]{1,0:T(1,128)S(1)}) custom-call(s32[1,256]{1,0:T(1,128)} %refs_0_.2, s32[1,256]{1,0:T(1,128)} %refs_0_.3, s32[1,256]{1,0:T(1,128)} %refs_2_.1, f32[256,4096]{1,0:T(8,128)} %bitcast.14, f32[256,4096]{1,0:T(8,128)} %bitcast.15), custom_call_target="tpu_custom_call" | custom-call | flops 40000000 | bytes 12582912 | tf_op jit(solution)/shard_map/token_terms/pallas_call | solution.py:129
  8.9 0.0 copy-start
  8.9 0.0 collective-permute-done.refs_1_
  8.9 0.0 collective-permute-done.1.refs_2_
  8.9 0.5 collective-permute-done.2.refs_3_
  9.4 0.0 copy-done.1
  9.4 1.1 %collective-permute-start.3 = (s32[1,256]{1,0:T(1,128)S(1)}, s32[1,256]{1,0:T(1,128)S(1)}, u32[]{:S(2)}, u32[]{:S(2)}) collective-permute-start(s32[1,256]{1,0:T(1,128)S(1)} %added.1.refs_0_), channel_id=1, source_target_pairs={{0,32},{16,48},{32,0},{48,16},{64,96},{80,112},{96,64},{112,80},{1... | collective-permute-start | bytes 3080 | tf_op jit(solution)/shard_map/ppermute | solution.py:528
  10.5 2.2 %pack.1 = (f32[7040,128]{1,0:T(8,128)S(1)}, f32[8,256]{1,0:T(8,128)S(1)}) custom-call(s32[1,256]{1,0:T(1,128)S(1)} %get-tuple-element.75.refs_0_.refs_4_, s32[1,256]{1,0:T(1,128)S(1)} %copy-done.1, f32[8192,128]{1,0:T(8,128)S(1)} %get-tuple-element.77.refs_2_, f32[256,128]{1,0:T(8,128)S(1)} %get-tuple-element.46.refs_3_), custom_call_target="tpu_custom_call" | custom-call | flops 40000000 | bytes 7208960 | tf_op jit(solution)/shard_map/pack/pallas_call | solution.py:278
  12.7 0.3 collective-permute-done.3.refs_1_
  13.1 0.0 copy-done
  13.1 0.3 stamp.1
  13.4 51.3 %all_to_all.9 = f32[16,440,128]{2,1,0:T(8,128)S(1)} all-to-all(f32[16,440,128]{2,1,0:T(8,128)S(1)} %stamp.1), channel_id=1, replica_groups=mesh['gx_0'=4,'gx_1'=2,'gy_0'=4,'gy_1'=4] {'gy_0','gy_1'}, dimensions={0} | all-to-all | bytes 7208960 | tf_op jit(solution)/shard_map/all_to_all | solution.py:550
  64.8 3.3 %score.1 = (f32[8192,128]{1,0:T(8,128)}, f32[16,16]{1,0:T(8,128)}, f32[16,16]{1,0:T(8,128)}, f32[3,16,128]{2,1,0:T(8,128)S(1)}, s32[1,128]{1,0:T(1,128)}) custom-call(f32[7040,128]{1,0:T(8,128)S(1)} %bitcast.12), custom_call_target="tpu_custom_call" | custom-call | tf_op jit(solution)/shard_map/score/pallas_call | solution.py:432
  68.1 0.7 %while.9 = (f32[8192,128]{1,0:T(8,128)}, s32[]{:T(128)}, s32[1,256]{1,0:T(1,128)S(1)}, s32[1,256]{1,0:T(1,128)S(1)}, f32[8192,128]{1,0:T(8,128)}, /*index=5*/f32[3,16,128]{2,1,0:T(8,128)S(1)}) while((f32[8192,128]{1,0:T(8,128)}, s32[]{:T(128)}, s32[1,256]{1,0:T(1,128)S(1)}, s32[1,256]{1,0:T(1,128)S(1)}, f32[8192,128]{1,0:T(8,128)}, ...), condition=%region_1.0_spmd, body=%region_0.0_spmd | while | flops 1 | bytes 1966177 | solution.py:559
  (1 shorter events, 0.0 us)
Async XLA Ops:
  0.6 8.3 %collective-permute-start = (s32[1,256]{1,0:T(1,128)}, s32[1,256]{1,0:T(1,128)S(1)}, u32[]{:S(2)}, u32[]{:S(2)}) collective-permute-start(s32[1,256]{1,0:T(1,128)} %refs_0_.3), channel_id=1, source_target_pairs={{0,64},{16,80},{32,96},{48,112},{64,0},{80,16},{96,32},{112,48},{1... | collective-permute-start | bytes 3080 | tf_op jit(solution)/shard_map/ppermute | solution.py:528
  4.7 4.2 %collective-permute-start.1 = (s32[1,256]{1,0:T(1,128)}, s32[1,256]{1,0:T(1,128)S(1)}, u32[]{:S(2)}, u32[]{:S(2)}) collective-permute-start(s32[1,256]{1,0:T(1,128)} %refs_0_.3), channel_id=1, source_target_pairs={{0,16},{16,0},{32,48},{48,32},{64,80},{80,64},{96,112},{112,96},{1... | collective-permute-start | bytes 3080 | tf_op jit(solution)/shard_map/ppermute | solution.py:528
  4.7 4.7 %collective-permute-start.2 = (s32[1,256]{1,0:T(1,128)}, s32[1,256]{1,0:T(1,128)S(1)}, u32[]{:S(2)}, u32[]{:S(2)}) collective-permute-start(s32[1,256]{1,0:T(1,128)} %refs_0_.3), channel_id=1, source_target_pairs={{0,80},{16,64},{32,112},{48,96},{64,16},{80,0},{96,48},{112,32},{1... | collective-permute-start | bytes 3080 | tf_op jit(solution)/shard_map/ppermute | solution.py:528
  4.9 4.5 %copy-start.1 = (s32[1,256]{1,0:T(1,128)S(1)}, s32[1,256]{1,0:T(1,128)}, u32[]{:S(2)}) copy-start(s32[1,256]{1,0:T(1,128)} %refs_0_.3) | copy-start | bytes 3076
  8.9 4.2 %copy-start = (f32[8192,128]{1,0:T(8,128)}, f32[8192,128]{1,0:T(8,128)S(1)}, u32[]{:S(2)}) copy-start(f32[8192,128]{1,0:T(8,128)S(1)} %get-tuple-element.77.refs_2_) | copy-start | bytes 12582916
  9.4 3.7 %collective-permute-start.3 = (s32[1,256]{1,0:T(1,128)S(1)}, s32[1,256]{1,0:T(1,128)S(1)}, u32[]{:S(2)}, u32[]{:S(2)}) collective-permute-start(s32[1,256]{1,0:T(1,128)S(1)} %added.1.refs_0_), channel_id=1, source_target_pairs={{0,32},{16,48},{32,0},{48,16},{64,96},{80,112},{96,64},{112,80},{1... | collective-permute-start | bytes 3080 | tf_op jit(solution)/shard_map/ppermute | solution.py:528

commit v6 on v5

--- a/solution.py
+++ b/solution.py
@@ -23,7 +23,7 @@
 
 SPAN = LANES // 4
 LEN, SUM_P, REWARD, SUM_Q = (i * SPAN for i in range(4))
-STEPS = 8
+STEPS = 16
 
 
 def token_kernel(
@@ -536,7 +536,7 @@
     members = members_dev * dests
     samples = members * slots * lax.axis_size(GX)
     scales = (float(samples * seq_slots), float(samples))
-    near = [lengths] + [partner(lengths, step) for step in (4, 1, 5)]
+    near = [lengths] + [partner(lengths, step) for step in (5, 4, 1)]
     u, sums, slot_of = token_terms(
         *(
             pltpu.with_memory_space_constraint(x, pltpu.HBM)

time: 68.9 us -> 68.4 us (level)
  no operation moved by 1% of the time
where the time goes in v6:
time: 68.4 us; the launch traced here: 68.2 us
  blocking collectives  50.8 us (74%)
  Pallas kernels  9.81 us (14%)
  starting transfers between devices  5.28 us (8%)
  waiting for transfers between devices  0.94 us (1%)
  loops' own time  0.69 us (1%)
    all_to_all x1, blocking collectives, body(): main = lax.all_to_all(main, GY, 0, 0, tiled=True)  50.8 us
    ppermute x4, starting transfers between devices, partner(): return lax.ppermute(x, GX, [(i, i ^ step) for i in range(size)])  5.28 us
    pallas_call x1, Pallas kernels, token_terms(): pl.pallas_call(body, out_shape=(jax.ShapeDtypeStruct((slots * width // LA...  4.01 us
    pallas_call x1, Pallas kernels, score(): pl.pallas_call(body, out_shape=(jax.ShapeDtypeStruct((members * full, LAN...  3.28 us
    pallas_call x1, Pallas kernels, pack(): pl.pallas_call(body, out_shape=(jax.ShapeDtypeStruct((dests * chunk, LANE...  2.19 us
  transfers between devices with their start and end apart: 4, of which 2 were waited for; matrix products, arithmetic and copies ran while one was open for 0% of the time, Pallas kernels for 9%

profile of v6, /device:TPU:0, one launch (start us, length us, event | category | flops | bytes accessed | tf_op | source)
XLA Modules:
  0.0 68.2 jit_solution(17943128137921067697)
XLA Ops:
  0.6 3.5 %collective-permute-start = (s32[1,256]{1,0:T(1,128)}, s32[1,256]{1,0:T(1,128)S(1)}, u32[]{:S(2)}, u32[]{:S(2)}) collective-permute-start(s32[1,256]{1,0:T(1,128)} %refs_0_.3), channel_id=1, source_target_pairs={{0,80},{16,64},{32,112},{48,96},{64,16},{80,0},{96,48},{112,32},{1... | collective-permute-start | bytes 3080 | tf_op jit(solution)/shard_map/ppermute | solution.py:528
  4.1 0.7 collective-permute-start.1
  4.8 0.0 collective-permute-start.2
  4.8 0.0 copy-start.1
  4.8 4.0 %token_terms.1 = (f32[8192,128]{1,0:T(8,128)S(1)}, f32[256,128]{1,0:T(8,128)S(1)}, s32[1,256]{1,0:T(1,128)S(1)}) custom-call(s32[1,256]{1,0:T(1,128)} %refs_0_.2, s32[1,256]{1,0:T(1,128)} %refs_0_.3, s32[1,256]{1,0:T(1,128)} %refs_2_.1, f32[256,4096]{1,0:T(8,128)} %bitcast.14, f32[256,4096]{1,0:T(8,128)} %bitcast.15), custom_call_target="tpu_custom_call" | custom-call | flops 40000000 | bytes 12582912 | tf_op jit(solution)/shard_map/token_terms/pallas_call | solution.py:129
  8.8 0.0 copy-start
  8.8 0.0 collective-permute-done.refs_1_
  8.9 0.6 collective-permute-done.1.refs_2_
  9.4 0.0 collective-permute-done.2.refs_3_
  9.4 0.0 copy-done.1
  9.4 1.1 %collective-permute-start.3 = (s32[1,256]{1,0:T(1,128)S(1)}, s32[1,256]{1,0:T(1,128)S(1)}, u32[]{:S(2)}, u32[]{:S(2)}) collective-permute-start(s32[1,256]{1,0:T(1,128)S(1)} %added.1.refs_0_), channel_id=1, source_target_pairs={{0,32},{16,48},{32,0},{48,16},{64,96},{80,112},{96,64},{112,80},{1... | collective-permute-start | bytes 3080 | tf_op jit(solution)/shard_map/ppermute | solution.py:528
  10.5 2.2 %pack.1 = (f32[7040,128]{1,0:T(8,128)S(1)}, f32[8,256]{1,0:T(8,128)S(1)}) custom-call(s32[1,256]{1,0:T(1,128)S(1)} %get-tuple-element.75.refs_0_.refs_4_, s32[1,256]{1,0:T(1,128)S(1)} %copy-done.1, f32[8192,128]{1,0:T(8,128)S(1)} %get-tuple-element.77.refs_2_, f32[256,128]{1,0:T(8,128)S(1)} %get-tuple-element.46.refs_3_), custom_call_target="tpu_custom_call" | custom-call | flops 40000000 | bytes 7208960 | tf_op jit(solution)/shard_map/pack/pallas_call | solution.py:278
  12.7 0.4 collective-permute-done.3.refs_1_
  13.1 0.0 copy-done
  13.1 0.3 stamp.1
  13.4 50.8 %all_to_all.9 = f32[16,440,128]{2,1,0:T(8,128)S(1)} all-to-all(f32[16,440,128]{2,1,0:T(8,128)S(1)} %stamp.1), channel_id=1, replica_groups=mesh['gx_0'=4,'gx_1'=2,'gy_0'=4,'gy_1'=4] {'gy_0','gy_1'}, dimensions={0} | all-to-all | bytes 7208960 | tf_op jit(solution)/shard_map/all_to_all | solution.py:550
  64.3 3.3 %score.1 = (f32[8192,128]{1,0:T(8,128)}, f32[16,16]{1,0:T(8,128)}, f32[16,16]{1,0:T(8,128)}, f32[3,16,128]{2,1,0:T(8,128)S(1)}, s32[1,128]{1,0:T(1,128)}) custom-call(f32[7040,128]{1,0:T(8,128)S(1)} %bitcast.12), custom_call_target="tpu_custom_call" | custom-call | tf_op jit(solution)/shard_map/score/pallas_call | solution.py:432
  67.5 0.7 %while.9 = (f32[8192,128]{1,0:T(8,128)}, s32[]{:T(128)}, s32[1,256]{1,0:T(1,128)S(1)}, s32[1,256]{1,0:T(1,128)S(1)}, f32[8192,128]{1,0:T(8,128)}, /*index=5*/f32[3,16,128]{2,1,0:T(8,128)S(1)}) while((f32[8192,128]{1,0:T(8,128)}, s32[]{:T(128)}, s32[1,256]{1,0:T(1,128)S(1)}, s32[1,256]{1,0:T(1,128)S(1)}, f32[8192,128]{1,0:T(8,128)}, ...), condition=%region_1.0_spmd, body=%region_0.0_spmd | while | flops 1 | bytes 1966177 | solution.py:559
  (1 shorter events, 0.0 us)
Async XLA Ops:
  0.6 8.2 %collective-permute-start = (s32[1,256]{1,0:T(1,128)}, s32[1,256]{1,0:T(1,128)S(1)}, u32[]{:S(2)}, u32[]{:S(2)}) collective-permute-start(s32[1,256]{1,0:T(1,128)} %refs_0_.3), channel_id=1, source_target_pairs={{0,80},{16,64},{32,112},{48,96},{64,16},{80,0},{96,48},{112,32},{1... | collective-permute-start | bytes 3080 | tf_op jit(solution)/shard_map/ppermute | solution.py:528
  4.1 5.3 %collective-permute-start.1 = (s32[1,256]{1,0:T(1,128)}, s32[1,256]{1,0:T(1,128)S(1)}, u32[]{:S(2)}, u32[]{:S(2)}) collective-permute-start(s32[1,256]{1,0:T(1,128)} %refs_0_.3), channel_id=1, source_target_pairs={{0,64},{16,80},{32,96},{48,112},{64,0},{80,16},{96,32},{112,48},{1... | collective-permute-start | bytes 3080 | tf_op jit(solution)/shard_map/ppermute | solution.py:528
  4.8 4.6 %collective-permute-start.2 = (s32[1,256]{1,0:T(1,128)}, s32[1,256]{1,0:T(1,128)S(1)}, u32[]{:S(2)}, u32[]{:S(2)}) collective-permute-start(s32[1,256]{1,0:T(1,128)} %refs_0_.3), channel_id=1, source_target_pairs={{0,16},{16,0},{32,48},{48,32},{64,80},{80,64},{96,112},{112,96},{1... | collective-permute-start | bytes 3080 | tf_op jit(solution)/shard_map/ppermute | solution.py:528
  4.8 4.6 %copy-start.1 = (s32[1,256]{1,0:T(1,128)S(1)}, s32[1,256]{1,0:T(1,128)}, u32[]{:S(2)}) copy-start(s32[1,256]{1,0:T(1,128)} %refs_0_.3) | copy-start | bytes 3076
  8.8 4.3 %copy-start = (f32[8192,128]{1,0:T(8,128)}, f32[8192,128]{1,0:T(8,128)S(1)}, u32[]{:S(2)}) copy-start(f32[8192,128]{1,0:T(8,128)S(1)} %get-tuple-element.77.refs_2_) | copy-start | bytes 12582916
  9.4 3.7 %collective-permute-start.3 = (s32[1,256]{1,0:T(1,128)S(1)}, s32[1,256]{1,0:T(1,128)S(1)}, u32[]{:S(2)}, u32[]{:S(2)}) collective-permute-start(s32[1,256]{1,0:T(1,128)S(1)} %added.1.refs_0_), channel_id=1, source_target_pairs={{0,32},{16,48},{32,0},{48,16},{64,96},{80,112},{96,64},{112,80},{1... | collective-permute-start | bytes 3080 | tf_op jit(solution)/shard_map/ppermute | solution.py:528

commit v7 on v6

--- a/solution.py
+++ b/solution.py
@@ -21,6 +21,7 @@
     return row * LANES + lax.broadcasted_iota(jnp.int32, (cols, LANES), 1)
 
 
+LEAST = 512
 SPAN = LANES // 4
 LEN, SUM_P, REWARD, SUM_Q = (i * SPAN for i in range(4))
 STEPS = 16
@@ -101,11 +102,15 @@
                 at = (pl.ds(first, 8), pl.ds(c * LANES, LANES))
                 a = policy[at]
                 d = anchor[at] - a
-                valid = behind < -c * LANES
                 u = jnp.exp(d) - 1.0
                 u_ref[pl.ds(first * cols + c // 8 * 64 + c % 8, 8, stride=8), :] = u
-                sums_q[c % 4] = sums_q[c % 4] + jnp.where(valid, u - d, 0.0)
-                sums_p[c % 4] = sums_p[c % 4] + jnp.where(valid, a, 0.0)
+                q = u - d
+                if (c + 1) * LANES > LEAST:
+                    valid = behind < -c * LANES
+                    q = jnp.where(valid, q, 0.0)
+                    a = jnp.where(valid, a, 0.0)
+                sums_q[c % 4] = sums_q[c % 4] + q
+                sums_p[c % 4] = sums_p[c % 4] + a
             parts[0, pl.ds(first, 8), :] = (sums_p[0] + sums_p[1]) + (sums_p[2] + sums_p[3])
             parts[1, pl.ds(first, 8), :] = (sums_q[0] + sums_q[1]) + (sums_q[2] + sums_q[3])
 

time: 68.4 us -> 68.4 us (level)
  no operation moved by 1% of the time
where the time goes in v7:
time: 68.4 us; the launch traced here: 68.2 us
  blocking collectives  50.8 us (74%)
  Pallas kernels  9.81 us (14%)
  starting transfers between devices  5.28 us (8%)
  waiting for transfers between devices  0.95 us (1%)
  loops' own time  0.69 us (1%)
    all_to_all x1, blocking collectives, body(): main = lax.all_to_all(main, GY, 0, 0, tiled=True)  50.8 us
    ppermute x4, starting transfers between devices, partner(): return lax.ppermute(x, GX, [(i, i ^ step) for i in range(size)])  5.28 us
    pallas_call x1, Pallas kernels, token_terms(): pl.pallas_call(body, out_shape=(jax.ShapeDtypeStruct((slots * width // LA...  4.01 us
    pallas_call x1, Pallas kernels, score(): pl.pallas_call(body, out_shape=(jax.ShapeDtypeStruct((members * full, LAN...  3.28 us
    pallas_call x1, Pallas kernels, pack(): pl.pallas_call(body, out_shape=(jax.ShapeDtypeStruct((dests * chunk, LANE...  2.19 us
  transfers between devices with their start and end apart: 4, of which 2 were waited for; matrix products, arithmetic and copies ran while one was open for 0% of the time, Pallas kernels for 9%

profile of v7, /device:TPU:0, one launch (start us, length us, event | category | flops | bytes accessed | tf_op | source)
XLA Modules:
  0.0 68.2 jit_solution(1095647893147899847)
XLA Ops:
  0.6 3.5 %collective-permute-start = (s32[1,256]{1,0:T(1,128)}, s32[1,256]{1,0:T(1,128)S(1)}, u32[]{:S(2)}, u32[]{:S(2)}) collective-permute-start(s32[1,256]{1,0:T(1,128)} %refs_0_.3), channel_id=1, source_target_pairs={{0,80},{16,64},{32,112},{48,96},{64,16},{80,0},{96,48},{112,32},{1... | collective-permute-start | bytes 3080 | tf_op jit(solution)/shard_map/ppermute | solution.py:533
  4.1 0.7 collective-permute-start.1
  4.8 0.0 collective-permute-start.2
  4.8 0.0 copy-start.1
  4.8 4.0 %token_terms.1 = (f32[8192,128]{1,0:T(8,128)S(1)}, f32[256,128]{1,0:T(8,128)S(1)}, s32[1,256]{1,0:T(1,128)S(1)}) custom-call(s32[1,256]{1,0:T(1,128)} %refs_0_.2, s32[1,256]{1,0:T(1,128)} %refs_0_.3, s32[1,256]{1,0:T(1,128)} %refs_2_.1, f32[256,4096]{1,0:T(8,128)} %bitcast.14, f32[256,4096]{1,0:T(8,128)} %bitcast.15), custom_call_target="tpu_custom_call" | custom-call | flops 40000000 | bytes 12582912 | tf_op jit(solution)/shard_map/token_terms/pallas_call | solution.py:134
  8.8 0.0 copy-start
  8.8 0.0 collective-permute-done.refs_1_
  8.9 0.6 collective-permute-done.1.refs_2_
  9.4 0.0 collective-permute-done.2.refs_3_
  9.4 0.0 copy-done.1
  9.4 1.1 %collective-permute-start.3 = (s32[1,256]{1,0:T(1,128)S(1)}, s32[1,256]{1,0:T(1,128)S(1)}, u32[]{:S(2)}, u32[]{:S(2)}) collective-permute-start(s32[1,256]{1,0:T(1,128)S(1)} %added.1.refs_0_), channel_id=1, source_target_pairs={{0,32},{16,48},{32,0},{48,16},{64,96},{80,112},{96,64},{112,80},{1... | collective-permute-start | bytes 3080 | tf_op jit(solution)/shard_map/ppermute | solution.py:533
  10.5 2.2 %pack.1 = (f32[7040,128]{1,0:T(8,128)S(1)}, f32[8,256]{1,0:T(8,128)S(1)}) custom-call(s32[1,256]{1,0:T(1,128)S(1)} %get-tuple-element.75.refs_0_.refs_4_, s32[1,256]{1,0:T(1,128)S(1)} %copy-done.1, f32[8192,128]{1,0:T(8,128)S(1)} %get-tuple-element.77.refs_2_, f32[256,128]{1,0:T(8,128)S(1)} %get-tuple-element.46.refs_3_), custom_call_target="tpu_custom_call" | custom-call | flops 40000000 | bytes 7208960 | tf_op jit(solution)/shard_map/pack/pallas_call | solution.py:283
  12.7 0.4 collective-permute-done.3.refs_1_
  13.1 0.0 copy-done
  13.1 0.3 stamp.1
  13.4 50.8 %all_to_all.9 = f32[16,440,128]{2,1,0:T(8,128)S(1)} all-to-all(f32[16,440,128]{2,1,0:T(8,128)S(1)} %stamp.1), channel_id=1, replica_groups=mesh['gx_0'=4,'gx_1'=2,'gy_0'=4,'gy_1'=4] {'gy_0','gy_1'}, dimensions={0} | all-to-all | bytes 7208960 | tf_op jit(solution)/shard_map/all_to_all | solution.py:555
  64.3 3.3 %score.1 = (f32[8192,128]{1,0:T(8,128)}, f32[16,16]{1,0:T(8,128)}, f32[16,16]{1,0:T(8,128)}, f32[3,16,128]{2,1,0:T(8,128)S(1)}, s32[1,128]{1,0:T(1,128)}) custom-call(f32[7040,128]{1,0:T(8,128)S(1)} %bitcast.12), custom_call_target="tpu_custom_call" | custom-call | tf_op jit(solution)/shard_map/score/pallas_call | solution.py:437
  67.5 0.7 %while.9 = (f32[8192,128]{1,0:T(8,128)}, s32[]{:T(128)}, s32[1,256]{1,0:T(1,128)S(1)}, s32[1,256]{1,0:T(1,128)S(1)}, f32[8192,128]{1,0:T(8,128)}, /*index=5*/f32[3,16,128]{2,1,0:T(8,128)S(1)}) while((f32[8192,128]{1,0:T(8,128)}, s32[]{:T(128)}, s32[1,256]{1,0:T(1,128)S(1)}, s32[1,256]{1,0:T(1,128)S(1)}, f32[8192,128]{1,0:T(8,128)}, ...), condition=%region_1.0_spmd, body=%region_0.0_spmd | while | flops 1 | bytes 1966177 | solution.py:564
  (1 shorter events, 0.0 us)
Async XLA Ops:
  0.6 8.2 %collective-permute-start = (s32[1,256]{1,0:T(1,128)}, s32[1,256]{1,0:T(1,128)S(1)}, u32[]{:S(2)}, u32[]{:S(2)}) collective-permute-start(s32[1,256]{1,0:T(1,128)} %refs_0_.3), channel_id=1, source_target_pairs={{0,80},{16,64},{32,112},{48,96},{64,16},{80,0},{96,48},{112,32},{1... | collective-permute-start | bytes 3080 | tf_op jit(solution)/shard_map/ppermute | solution.py:533
  4.1 5.3 %collective-permute-start.1 = (s32[1,256]{1,0:T(1,128)}, s32[1,256]{1,0:T(1,128)S(1)}, u32[]{:S(2)}, u32[]{:S(2)}) collective-permute-start(s32[1,256]{1,0:T(1,128)} %refs_0_.3), channel_id=1, source_target_pairs={{0,64},{16,80},{32,96},{48,112},{64,0},{80,16},{96,32},{112,48},{1... | collective-permute-start | bytes 3080 | tf_op jit(solution)/shard_map/ppermute | solution.py:533
  4.8 4.6 %collective-permute-start.2 = (s32[1,256]{1,0:T(1,128)}, s32[1,256]{1,0:T(1,128)S(1)}, u32[]{:S(2)}, u32[]{:S(2)}) collective-permute-start(s32[1,256]{1,0:T(1,128)} %refs_0_.3), channel_id=1, source_target_pairs={{0,16},{16,0},{32,48},{48,32},{64,80},{80,64},{96,112},{112,96},{1... | collective-permute-start | bytes 3080 | tf_op jit(solution)/shard_map/ppermute | solution.py:533
  4.8 4.6 %copy-start.1 = (s32[1,256]{1,0:T(1,128)S(1)}, s32[1,256]{1,0:T(1,128)}, u32[]{:S(2)}) copy-start(s32[1,256]{1,0:T(1,128)} %refs_0_.3) | copy-start | bytes 3076
  8.8 4.3 %copy-start = (f32[8192,128]{1,0:T(8,128)}, f32[8192,128]{1,0:T(8,128)S(1)}, u32[]{:S(2)}) copy-start(f32[8192,128]{1,0:T(8,128)S(1)} %get-tuple-element.77.refs_2_) | copy-start | bytes 12582916
  9.4 3.7 %collective-permute-start.3 = (s32[1,256]{1,0:T(1,128)S(1)}, s32[1,256]{1,0:T(1,128)S(1)}, u32[]{:S(2)}, u32[]{:S(2)}) collective-permute-start(s32[1,256]{1,0:T(1,128)S(1)} %added.1.refs_0_), channel_id=1, source_target_pairs={{0,32},{16,48},{32,0},{48,16},{64,96},{80,112},{96,64},{112,80},{1... | collective-permute-start | bytes 3080 | tf_op jit(solution)/shard_map/ppermute | solution.py:533

commit v8 on v7

--- a/solution.py
+++ b/solution.py
@@ -84,7 +84,7 @@
         for load in loads(step):
             load.wait()
 
-        @pl.loop(0, rows // 8)
+        @pl.loop(0, rows // 8, unroll=2)
         def _(group):
             first = pl.multiple_of(step * rows + group * 8, 8)
             length = jnp.full((8, LANES), len_ref[0, first], jnp.int32)

time: 68.4 us -> 68.4 us (level)
  no operation moved by 1% of the time
where the time goes in v8:
time: 68.4 us; the launch traced here: 68.2 us
  blocking collectives  50.8 us (74%)
  Pallas kernels  9.8 us (14%)
  starting transfers between devices  5.28 us (8%)
  waiting for transfers between devices  0.95 us (1%)
  loops' own time  0.69 us (1%)
    all_to_all x1, blocking collectives, body(): main = lax.all_to_all(main, GY, 0, 0, tiled=True)  50.8 us
    ppermute x4, starting transfers between devices, partner(): return lax.ppermute(x, GX, [(i, i ^ step) for i in range(size)])  5.28 us
    pallas_call x1, Pallas kernels, token_terms(): pl.pallas_call(body, out_shape=(jax.ShapeDtypeStruct((slots * width // LA...  4 us
    pallas_call x1, Pallas kernels, score(): pl.pallas_call(body, out_shape=(jax.ShapeDtypeStruct((members * full, LAN...  3.28 us
    pallas_call x1, Pallas kernels, pack(): pl.pallas_call(body, out_shape=(jax.ShapeDtypeStruct((dests * chunk, LANE...  2.19 us
  transfers between devices with their start and end apart: 4, of which 2 were waited for; matrix products, arithmetic and copies ran while one was open for 0% of the time, Pallas kernels for 9%

profile of v8, /device:TPU:0, one launch (start us, length us, event | category | flops | bytes accessed | tf_op | source)
XLA Modules:
  0.0 68.2 jit_solution(10589816483621183992)
XLA Ops:
  0.6 3.5 %collective-permute-start = (s32[1,256]{1,0:T(1,128)}, s32[1,256]{1,0:T(1,128)S(1)}, u32[]{:S(2)}, u32[]{:S(2)}) collective-permute-start(s32[1,256]{1,0:T(1,128)} %refs_0_.3), channel_id=1, source_target_pairs={{0,80},{16,64},{32,112},{48,96},{64,16},{80,0},{96,48},{112,32},{1... | collective-permute-start | bytes 3080 | tf_op jit(solution)/shard_map/ppermute | solution.py:533
  4.1 0.7 collective-permute-start.1
  4.8 0.0 collective-permute-start.2
  4.8 0.0 copy-start.1
  4.8 4.0 %token_terms.1 = (f32[8192,128]{1,0:T(8,128)S(1)}, f32[256,128]{1,0:T(8,128)S(1)}, s32[1,256]{1,0:T(1,128)S(1)}) custom-call(s32[1,256]{1,0:T(1,128)} %refs_0_.2, s32[1,256]{1,0:T(1,128)} %refs_0_.3, s32[1,256]{1,0:T(1,128)} %refs_2_.1, f32[256,4096]{1,0:T(8,128)} %bitcast.14, f32[256,4096]{1,0:T(8,128)} %bitcast.15), custom_call_target="tpu_custom_call" | custom-call | flops 40000000 | bytes 12582912 | tf_op jit(solution)/shard_map/token_terms/pallas_call | solution.py:134
  8.8 0.0 copy-start
  8.8 0.0 collective-permute-done.refs_1_
  8.8 0.6 collective-permute-done.1.refs_2_
  9.4 0.0 collective-permute-done.2.refs_3_
  9.4 0.0 copy-done.1
  9.4 1.1 %collective-permute-start.3 = (s32[1,256]{1,0:T(1,128)S(1)}, s32[1,256]{1,0:T(1,128)S(1)}, u32[]{:S(2)}, u32[]{:S(2)}) collective-permute-start(s32[1,256]{1,0:T(1,128)S(1)} %added.1.refs_0_), channel_id=1, source_target_pairs={{0,32},{16,48},{32,0},{48,16},{64,96},{80,112},{96,64},{112,80},{1... | collective-permute-start | bytes 3080 | tf_op jit(solution)/shard_map/ppermute | solution.py:533
  10.5 2.2 %pack.1 = (f32[7040,128]{1,0:T(8,128)S(1)}, f32[8,256]{1,0:T(8,128)S(1)}) custom-call(s32[1,256]{1,0:T(1,128)S(1)} %get-tuple-element.75.refs_0_.refs_4_, s32[1,256]{1,0:T(1,128)S(1)} %copy-done.1, f32[8192,128]{1,0:T(8,128)S(1)} %get-tuple-element.77.refs_2_, f32[256,128]{1,0:T(8,128)S(1)} %get-tuple-element.46.refs_3_), custom_call_target="tpu_custom_call" | custom-call | flops 40000000 | bytes 7208960 | tf_op jit(solution)/shard_map/pack/pallas_call | solution.py:283
  12.7 0.4 collective-permute-done.3.refs_1_
  13.1 0.0 copy-done
  13.1 0.3 stamp.1
  13.4 50.8 %all_to_all.9 = f32[16,440,128]{2,1,0:T(8,128)S(1)} all-to-all(f32[16,440,128]{2,1,0:T(8,128)S(1)} %stamp.1), channel_id=1, replica_groups=mesh['gx_0'=4,'gx_1'=2,'gy_0'=4,'gy_1'=4] {'gy_0','gy_1'}, dimensions={0} | all-to-all | bytes 7208960 | tf_op jit(solution)/shard_map/all_to_all | solution.py:555
  64.2 3.3 %score.1 = (f32[8192,128]{1,0:T(8,128)}, f32[16,16]{1,0:T(8,128)}, f32[16,16]{1,0:T(8,128)}, f32[3,16,128]{2,1,0:T(8,128)S(1)}, s32[1,128]{1,0:T(1,128)}) custom-call(f32[7040,128]{1,0:T(8,128)S(1)} %bitcast.12), custom_call_target="tpu_custom_call" | custom-call | tf_op jit(solution)/shard_map/score/pallas_call | solution.py:437
  67.5 0.7 %while.9 = (f32[8192,128]{1,0:T(8,128)}, s32[]{:T(128)}, s32[1,256]{1,0:T(1,128)S(1)}, s32[1,256]{1,0:T(1,128)S(1)}, f32[8192,128]{1,0:T(8,128)}, /*index=5*/f32[3,16,128]{2,1,0:T(8,128)S(1)}) while((f32[8192,128]{1,0:T(8,128)}, s32[]{:T(128)}, s32[1,256]{1,0:T(1,128)S(1)}, s32[1,256]{1,0:T(1,128)S(1)}, f32[8192,128]{1,0:T(8,128)}, ...), condition=%region_1.0_spmd, body=%region_0.0_spmd | while | flops 1 | bytes 1966177 | solution.py:564
  (1 shorter events, 0.0 us)
Async XLA Ops:
  0.6 8.2 %collective-permute-start = (s32[1,256]{1,0:T(1,128)}, s32[1,256]{1,0:T(1,128)S(1)}, u32[]{:S(2)}, u32[]{:S(2)}) collective-permute-start(s32[1,256]{1,0:T(1,128)} %refs_0_.3), channel_id=1, source_target_pairs={{0,80},{16,64},{32,112},{48,96},{64,16},{80,0},{96,48},{112,32},{1... | collective-permute-start | bytes 3080 | tf_op jit(solution)/shard_map/ppermute | solution.py:533
  4.1 5.3 %collective-permute-start.1 = (s32[1,256]{1,0:T(1,128)}, s32[1,256]{1,0:T(1,128)S(1)}, u32[]{:S(2)}, u32[]{:S(2)}) collective-permute-start(s32[1,256]{1,0:T(1,128)} %refs_0_.3), channel_id=1, source_target_pairs={{0,64},{16,80},{32,96},{48,112},{64,0},{80,16},{96,32},{112,48},{1... | collective-permute-start | bytes 3080 | tf_op jit(solution)/shard_map/ppermute | solution.py:533
  4.8 4.6 %collective-permute-start.2 = (s32[1,256]{1,0:T(1,128)}, s32[1,256]{1,0:T(1,128)S(1)}, u32[]{:S(2)}, u32[]{:S(2)}) collective-permute-start(s32[1,256]{1,0:T(1,128)} %refs_0_.3), channel_id=1, source_target_pairs={{0,16},{16,0},{32,48},{48,32},{64,80},{80,64},{96,112},{112,96},{1... | collective-permute-start | bytes 3080 | tf_op jit(solution)/shard_map/ppermute | solution.py:533
  4.8 4.6 %copy-start.1 = (s32[1,256]{1,0:T(1,128)S(1)}, s32[1,256]{1,0:T(1,128)}, u32[]{:S(2)}) copy-start(s32[1,256]{1,0:T(1,128)} %refs_0_.3) | copy-start | bytes 3076
  8.8 4.3 %copy-start = (f32[8192,128]{1,0:T(8,128)}, f32[8192,128]{1,0:T(8,128)S(1)}, u32[]{:S(2)}) copy-start(f32[8192,128]{1,0:T(8,128)S(1)} %get-tuple-element.77.refs_2_) | copy-start | bytes 12582916
  9.4 3.7 %collective-permute-start.3 = (s32[1,256]{1,0:T(1,128)S(1)}, s32[1,256]{1,0:T(1,128)S(1)}, u32[]{:S(2)}, u32[]{:S(2)}) collective-permute-start(s32[1,256]{1,0:T(1,128)S(1)} %added.1.refs_0_), channel_id=1, source_target_pairs={{0,32},{16,48},{32,0},{48,16},{64,96},{80,112},{96,64},{112,80},{1... | collective-permute-start | bytes 3080 | tf_op jit(solution)/shard_map/ppermute | solution.py:533
